TPU v7x, 32 devices: a whole 2x2x4 slice. The times are simulated.
32 devices in a mesh: dp: 8 (over z, x), mp: 4 (over y, core).
Axes of the slice: x: 2, y: 2, z: 4, core: 2. Of those that a mesh axis runs over, the one named last changes fastest.
Arguments:
- tokens: bfloat16 [16384, 1024], P(('dp', 'mp')), may hold values from -6 to 6
- lengths: int32 [8, 1], P('dp'), may hold values from 30 to 2048, as said below
- query_weight: bfloat16 [1024, 1024], P(None, 'mp'), may hold values from -0.25 to 0.25
- query_bias: bfloat16 [1024], P('mp'), may hold values from -3 to 3
- key_weight: bfloat16 [1024, 1024], P(None, 'mp'), may hold values from -0.25 to 0.25
- value_weight: bfloat16 [1024, 1024], P(None, 'mp'), may hold values from -0.1875 to 0.1875
- value_bias: bfloat16 [1024], P('mp'), may hold values from -3 to 3
- out_weight: bfloat16 [1024, 1024], P('mp'), may hold values from -0.75 to 0.75
- out_bias: bfloat16 [1024], replicated, may hold values from -3 to 3
- first_gain: bfloat16 [1024], replicated, may hold values from 0.25 to 1.75
- first_shift: bfloat16 [1024], replicated, may hold values from -3 to 3
- up_weight: bfloat16 [1024, 4096], P(None, 'mp'), may hold values from -0.1875 to 0.1875
- up_bias: bfloat16 [4096], P('mp'), may hold values from -3 to 3
- down_weight: bfloat16 [4096, 1024], P('mp'), may hold values from -0.09375 to 0.09375
- down_bias: bfloat16 [1024], replicated, may hold values from -3 to 3
- second_gain: bfloat16 [1024], replicated, may hold values from 0.25 to 1.75
- second_shift: bfloat16 [1024], replicated, may hold values from -3 to 3
- output_grad: bfloat16 [16384, 1024], P(('dp', 'mp')), may hold values from -6 to 6
Outputs:
- layer_out: bfloat16 [16384, 1024], P(('dp', 'mp'))
- tokens_grad: bfloat16 [16384, 1024], P(('dp', 'mp'))
- query_weight_grad: float32 [1024, 1024], P(None, 'mp')
- query_bias_grad: float32 [1024], P('mp')
- key_weight_grad: float32 [1024, 1024], P(None, 'mp')
- value_weight_grad: float32 [1024, 1024], P(None, 'mp')
- value_bias_grad: float32 [1024], P('mp')
- out_weight_grad: float32 [1024, 1024], P('mp')
- out_bias_grad: float32 [1024], replicated
- first_gain_grad: float32 [1024], replicated
- first_shift_grad: float32 [1024], replicated
- up_weight_grad: float32 [1024, 4096], P(None, 'mp')
- up_bias_grad: float32 [4096], P('mp')
- down_weight_grad: float32 [4096, 1024], P('mp')
- down_bias_grad: float32 [1024], replicated
- second_gain_grad: float32 [1024], replicated
- second_shift_grad: float32 [1024], replicated
Inputs may be any that keep to these rules, and one draw needn't show every extreme that they name: Batch b holds 1 sequence of 2048 rows; sequence s counts its first lengths[b, s] rows as keys; in every draw some sequence has exactly 2048.
All inputs are finite; a program needn't handle non-finite values.
Results may differ from a plain program's by a relative error of at most 0.023.
Values may be sent and summed in bfloat16 or wider, within the bound.
A program may use at most 320 MiB of HBM per device.

v0:
```python
from functools import partial

import jax
import jax.numpy as jnp
from jax import lax
from jax.experimental import pallas as pl
from jax.experimental.pallas import tpu as pltpu
from jax.sharding import PartitionSpec as P

HD = 64


epsilon = 1e-12


def norm_forward(resid, gain, shift):
    center = resid - jnp.mean(resid, -1, keepdims=True)
    inv_std = lax.rsqrt(jnp.mean(center * center, -1, keepdims=True) + epsilon)
    normed = center * inv_std
    return (normed * gain + shift, normed, inv_std)


def norm_backward(grad, normed, inv_std, gain):
    scaled = grad * gain
    back = inv_std * (
        scaled
        - jnp.mean(scaled, -1, keepdims=True)
        - normed * jnp.mean(scaled * normed, -1, keepdims=True)
    )
    return (back, jnp.sum(grad * normed, 0), jnp.sum(grad, 0))


F32 = jnp.float32
BF = jnp.bfloat16
MASKED = -1000000000.0
WIDE = 2 * HD


def mm(a, b, ca, cb):
    return lax.dot_general(a, b, (((ca,), (cb,)), ((), ())), preferred_element_type=F32)


def forward_kernel(heads, len_ref, q_ref, k_ref, vt_ref, e_ref, o_ref, r_ref, v_aug, k_aug):
    seq, step = pl.program_id(0), pl.program_id(2)
    seq_len, block = k_ref.shape[0], q_ref.shape[0]

    @pl.when(step == 0)
    def _():
        rows = lax.broadcasted_iota(jnp.int32, (seq_len, WIDE), 0)
        lanes = lax.broadcasted_iota(jnp.int32, (seq_len, WIDE), 1)
        bias = jnp.where(rows < len_ref[seq], 0.0, MASKED)
        keys = k_ref[...].astype(F32)
        for h in range(heads):
            other = (1 - h) * HD
            k_aug[h] = jnp.where(
                lanes // HD == h, keys, jnp.where(lanes == other, bias, 0.0)
            ).astype(BF)
            v_aug[h, :HD] = vt_ref[h * HD : (h + 1) * HD, :]
            v_aug[h, HD:] = jnp.ones((16, seq_len), BF)

    query = q_ref[...].astype(F32) * HD**-0.5
    lanes = lax.broadcasted_iota(jnp.int32, (block, WIDE), 1)
    scores = []
    for h in range(heads):
        other = (1 - h) * HD
        q_aug = jnp.where(
            lanes // HD == h, query, jnp.where(lanes == other, 1.0, 0.0)
        ).astype(BF)
        scores.append(mm(k_aug[h], q_aug, 1, 1))
    outs = []
    for h in range(heads):
        top = jnp.max(scores[h], 0, keepdims=True)
        expon = jnp.exp(scores[h] - top).astype(BF)
        e_ref[h] = expon
        total = mm(v_aug[h], expon, 1, 0)
        inverse = 1.0 / total[HD : HD + 1]
        r_ref[h] = inverse
        outs.append(total[:HD] * inverse)
    if heads == 1:
        outs.append(jnp.zeros_like(outs[0]))
    o_ref[...] = jnp.concatenate(outs, 0).T.astype(BF)


def backward_kernel(
    heads, e_ref, r_ref, q_ref, k_ref, v_ref, o_ref, g_ref, dq_ref, dk_ref, dv_ref, v_aug, k_t, dks, dvs
):
    step, last = pl.program_id(2), pl.num_programs(2) - 1
    seq_len, block = k_ref.shape[0], q_ref.shape[0]

    @pl.when(step == 0)
    def _():
        lanes = lax.broadcasted_iota(jnp.int32, (seq_len, WIDE), 1)
        values = v_ref[...].astype(F32)
        for h in range(heads):
            other = (1 - h) * HD
            ones = jnp.where((lanes >= other) & (lanes < other + 2), 1.0, 0.0)
            v_aug[h] = jnp.where(lanes // HD == h, values, ones).astype(BF)
        k_t[...] = (k_ref[...].astype(F32) * HD**-0.5).T.astype(BF)
        dks[...] = jnp.zeros_like(dks)
        dvs[...] = jnp.zeros_like(dvs)

    lanes = lax.broadcasted_iota(jnp.int32, (block, WIDE), 1)
    inverse = jnp.concatenate(
        [jnp.broadcast_to(r_ref[h % heads], (HD, block)) for h in range(2)], 0
    ).T
    grad = (g_ref[...].astype(F32) * inverse).astype(BF)
    grad_wide = grad.astype(F32)
    scaled_query = (q_ref[...].astype(F32) * HD**-0.5).astype(BF)
    product = grad_wide * o_ref[...].astype(F32)
    centered = []
    for h in range(heads):
        other = (1 - h) * HD
        inside = lanes // HD == h
        row_dot = jnp.sum(jnp.where(inside, product, 0.0), -1, keepdims=True)
        high = row_dot.astype(BF).astype(F32)
        g_aug = jnp.where(
            inside,
            grad_wide,
            jnp.where(lanes == other, -high, jnp.where(lanes == other + 1, high - row_dot, 0.0)),
        ).astype(BF)
        centered.append(mm(v_aug[h], g_aug, 1, 1))
    query_grads = []
    for h in range(heads):
        cols = slice(h * HD, (h + 1) * HD)
        expon = e_ref[h]
        score_grad = (expon.astype(F32) * centered[h]).astype(BF)
        dvs[h] += mm(expon, grad[:, cols], 1, 0)
        dks[h] += mm(score_grad, scaled_query[:, cols], 1, 0)
        query_grads.append(mm(k_t[cols, :], score_grad, 1, 0))
    if heads == 1:
        query_grads.append(jnp.zeros_like(query_grads[0]))
    dq_ref[...] = jnp.concatenate(query_grads, 0).T.astype(BF)

    @pl.when(step == last)
    def _():
        for total, out in ((dks, dk_ref), (dvs, dv_ref)):
            halves = [total[h] for h in range(heads)]
            if heads == 1:
                halves.append(jnp.zeros_like(halves[0]))
            out[...] = jnp.concatenate(halves, 1).astype(BF)


def attention_shape(rows, cols, seqs):
    seq_len = rows // seqs
    block = min(512, seq_len)
    steps = seq_len // block
    pairs = max(1, cols // WIDE)
    heads = cols // HD // pairs
    row_spec = pl.BlockSpec((block, WIDE), lambda s, p, j, *_: (s * steps + j, p))
    key_spec = pl.BlockSpec((seq_len, WIDE), lambda s, p, j, *_: (s, p))
    e_spec = pl.BlockSpec((heads, seq_len, block), lambda s, p, j, *_: (p, s, j))
    r_spec = pl.BlockSpec((heads, 1, block), lambda s, p, j, *_: (p, 0, s * steps + j))
    return seq_len, heads, pairs, (seqs, pairs, steps), row_spec, key_spec, e_spec, r_spec


def widen(array):
    short = WIDE - array.shape[1]
    return array if short <= 0 else jnp.pad(array, ((0, 0), (0, short)))


def attention_forward(queries, keys, values, lengths):
    rows, cols = queries.shape
    seqs = lengths.shape[0]
    seq_len, heads, pairs, grid, row_spec, key_spec, e_spec, r_spec = attention_shape(rows, cols, seqs)
    wide_cols = pairs * WIDE
    expon, attended, inverse = pl.pallas_call(
        partial(forward_kernel, heads),
        grid_spec=pltpu.PrefetchScalarGridSpec(
            num_scalar_prefetch=1,
            grid=grid,
            in_specs=[
                row_spec,
                key_spec,
                pl.BlockSpec((WIDE, seq_len), lambda s, p, j, *_: (p, s)),
            ],
            out_specs=[e_spec, row_spec, r_spec],
            scratch_shapes=[
                pltpu.VMEM((heads, HD + 16, seq_len), BF),
                pltpu.VMEM((heads, seq_len, WIDE), BF),
            ],
        ),
        out_shape=[
            jax.ShapeDtypeStruct((heads * pairs, rows, seq_len), BF),
            jax.ShapeDtypeStruct((rows, wide_cols), BF),
            jax.ShapeDtypeStruct((heads * pairs, 1, rows), F32),
        ],
        name="attention_forward",
        compiler_params=pltpu.CompilerParams(vmem_limit_bytes=60 * 1024 * 1024),
    )(lengths, widen(queries), widen(keys), widen(values).T)
    return expon, attended[:, :cols], inverse


def attention_backward(expon, inverse, queries, keys, values, attended, grad, seqs):
    rows, cols = queries.shape
    seq_len, heads, pairs, grid, row_spec, key_spec, e_spec, r_spec = attention_shape(rows, cols, seqs)
    shape = jax.ShapeDtypeStruct((rows, pairs * WIDE), BF)
    outs = pl.pallas_call(
        partial(backward_kernel, heads),
        grid=grid,
        in_specs=[e_spec, r_spec, row_spec, key_spec, key_spec, row_spec, row_spec],
        out_specs=[row_spec, key_spec, key_spec],
        scratch_shapes=[
            pltpu.VMEM((heads, seq_len, WIDE), BF),
            pltpu.VMEM((WIDE, seq_len), BF),
            pltpu.VMEM((heads, seq_len, HD), F32),
            pltpu.VMEM((heads, seq_len, HD), F32),
        ],
        out_shape=[shape] * 3,
        name="attention_backward",
        compiler_params=pltpu.CompilerParams(vmem_limit_bytes=60 * 1024 * 1024),
    )(expon, inverse, *[widen(x) for x in (queries, keys, values, attended, grad)])
    return [x[:, :cols] for x in outs]


def contract_rows(left, right):
    return lax.dot_general(
        left, right, (((0,), (0,)), ((), ())), preferred_element_type=jnp.float32
    )


def contract_cols(left, right):
    return lax.dot_general(
        left, right, (((1,), (1,)), ((), ())), preferred_element_type=jnp.float32
    )


def split_projection(projected, width, q_bias, v_bias):
    query_part = (projected[:, :width] + q_bias).astype(jnp.bfloat16)
    key_part = projected[:, width : 2 * width].astype(jnp.bfloat16)
    value_part = (projected[:, 2 * width :] + v_bias).astype(jnp.bfloat16)
    return (query_part, key_part, value_part)


def per_device_general(
    tokens,
    lengths,
    query_weight,
    query_bias,
    key_weight,
    value_weight,
    value_bias,
    out_weight,
    out_bias,
    first_gain,
    first_shift,
    up_weight,
    up_bias,
    down_weight,
    down_bias,
    second_gain,
    second_shift,
    output_grad,
):
    local_rows = tokens.shape[0]
    head_cols = query_weight.shape[1]
    seq_count = lengths.shape[1]
    all_rows = local_rows * lax.axis_size("mp")
    gathered = lax.all_gather(tokens, "mp", axis=0, tiled=True)
    joint_weight = jnp.concatenate([query_weight, key_weight, value_weight], 1)
    projected = jnp.dot(gathered, joint_weight, preferred_element_type=jnp.float32)
    queries, key_rows, values = split_projection(projected, head_cols, query_bias, value_bias)
    expon, attended, inverse = attention_forward(queries, key_rows, values, lengths[0])
    branch_one = lax.psum_scatter(
        jnp.dot(
            lax.slice_in_dim(attended, 0, local_rows * lax.axis_size("mp"), axis=0),
            out_weight,
            preferred_element_type=jnp.float32,
        ).astype(jnp.bfloat16),
        "mp",
        scatter_dimension=0,
        tiled=True,
    ).astype(jnp.float32)
    hidden, normed_one, inv_one = norm_forward(
        tokens.astype(jnp.float32) + branch_one + out_bias, first_gain, first_shift
    )
    hidden_low = hidden.astype(jnp.bfloat16)
    hidden_all = lax.all_gather(hidden_low, "mp", axis=0, tiled=True)
    pre_act = jnp.dot(hidden_all, up_weight, preferred_element_type=jnp.float32) + up_bias
    act_low = jax.nn.gelu(pre_act, approximate=False).astype(jnp.bfloat16)
    branch_two = lax.psum_scatter(
        jnp.dot(
            lax.slice_in_dim(act_low, 0, local_rows * lax.axis_size("mp"), axis=0),
            down_weight,
            preferred_element_type=jnp.float32,
        ).astype(jnp.bfloat16),
        "mp",
        scatter_dimension=0,
        tiled=True,
    ).astype(jnp.float32)
    layer_out, normed_two, inv_two = norm_forward(
        hidden + branch_two + down_bias, second_gain, second_shift
    )
    resid_two_grad, second_gain_grad, second_shift_grad = norm_backward(
        output_grad.astype(jnp.float32), normed_two, inv_two, second_gain
    )
    down_bias_grad = jnp.sum(resid_two_grad, 0)
    branch_two_low = resid_two_grad.astype(jnp.bfloat16)
    row_piece = lax.all_gather(branch_two_low, "mp", axis=0, tiled=True)
    row_start = jnp.int32(0)
    weight_acc = jnp.zeros(down_weight.shape, jnp.float32)
    act_acc = jnp.zeros(act_low.shape, jnp.float32)
    act_rows = lax.dynamic_slice_in_dim(act_low, row_start, row_piece.shape[0], 0)
    weight_acc = weight_acc + contract_rows(act_rows, row_piece)
    act_acc = lax.dynamic_update_slice_in_dim(
        act_acc, contract_cols(row_piece, down_weight), row_start, 0
    )
    down_weight_grad = weight_acc
    unused_two, gelu_back = jax.vjp(partial(jax.nn.gelu, approximate=False), pre_act)
    pre_grad = gelu_back(act_acc)[0].astype(jnp.bfloat16)
    up_bias_grad = jnp.sum(pre_grad, 0, dtype=jnp.float32)
    up_weight_grad = contract_rows(hidden_all, pre_grad)
    hidden_back = lax.psum_scatter(
        contract_cols(
            lax.slice_in_dim(pre_grad, 0, local_rows * lax.axis_size("mp"), axis=0), up_weight
        ).astype(jnp.bfloat16),
        "mp",
        scatter_dimension=0,
        tiled=True,
    ).astype(jnp.float32)
    hidden_grad = resid_two_grad + hidden_back
    resid_one_grad, first_gain_grad, first_shift_grad = norm_backward(
        hidden_grad, normed_one, inv_one, first_gain
    )
    out_bias_grad = jnp.sum(resid_one_grad, 0)
    branch_one_low = resid_one_grad.astype(jnp.bfloat16)
    row_piece = lax.all_gather(branch_one_low, "mp", axis=0, tiled=True)
    row_start = jnp.int32(0)
    weight_acc = jnp.zeros(out_weight.shape, jnp.float32)
    attn_acc = jnp.zeros(attended.shape, jnp.float32)
    attn_rows = lax.dynamic_slice_in_dim(attended, row_start, row_piece.shape[0], 0)
    weight_acc = weight_acc + contract_rows(attn_rows, row_piece)
    attn_acc = lax.dynamic_update_slice_in_dim(
        attn_acc, contract_cols(row_piece, out_weight), row_start, 0
    )
    out_weight_grad = weight_acc
    attn_low = attn_acc.astype(jnp.bfloat16)
    query_flat, key_flat, value_flat = attention_backward(
        expon, inverse, queries, key_rows, values, attended, attn_low, seq_count
    )
    width_now = query_flat.shape[1]
    joint_grad = jnp.concatenate([query_flat, key_flat, value_flat], 1)
    query_bias_grad = jnp.sum(query_flat, 0, dtype=jnp.float32)
    value_bias_grad = jnp.sum(value_flat, 0, dtype=jnp.float32)
    joint_weight_grad = contract_rows(gathered, joint_grad)
    input_back = lax.psum_scatter(
        contract_cols(
            lax.slice_in_dim(joint_grad, 0, local_rows * lax.axis_size("mp"), axis=0), joint_weight
        ).astype(jnp.bfloat16),
        "mp",
        scatter_dimension=0,
        tiled=True,
    ).astype(jnp.float32)
    tokens_grad = (resid_one_grad + input_back).astype(jnp.bfloat16)
    query_weight_grad = joint_weight_grad[:, :width_now]
    key_weight_grad = joint_weight_grad[:, width_now : 2 * width_now]
    value_weight_grad = joint_weight_grad[:, 2 * width_now :]
    (
        query_weight_grad,
        query_bias_grad,
        key_weight_grad,
        value_weight_grad,
        value_bias_grad,
        out_weight_grad,
        up_weight_grad,
        up_bias_grad,
        down_weight_grad,
    ) = (
        lax.psum(query_weight_grad.astype(jnp.bfloat16), "dp").astype(jnp.float32),
        lax.psum(query_bias_grad.astype(jnp.bfloat16), "dp").astype(jnp.float32),
        lax.psum(key_weight_grad.astype(jnp.bfloat16), "dp").astype(jnp.float32),
        lax.psum(value_weight_grad.astype(jnp.bfloat16), "dp").astype(jnp.float32),
        lax.psum(value_bias_grad.astype(jnp.bfloat16), "dp").astype(jnp.float32),
        lax.psum(out_weight_grad.astype(jnp.bfloat16), "dp").astype(jnp.float32),
        lax.psum(up_weight_grad.astype(jnp.bfloat16), "dp").astype(jnp.float32),
        lax.psum(up_bias_grad.astype(jnp.bfloat16), "dp").astype(jnp.float32),
        lax.psum(down_weight_grad.astype(jnp.bfloat16), "dp").astype(jnp.float32),
    )
    (
        out_bias_grad,
        first_gain_grad,
        first_shift_grad,
        down_bias_grad,
        second_gain_grad,
        second_shift_grad,
    ) = lax.psum(
        (
            out_bias_grad,
            first_gain_grad,
            first_shift_grad,
            down_bias_grad,
            second_gain_grad,
            second_shift_grad,
        ),
        ("dp", "mp"),
    )
    return (
        layer_out.astype(jnp.bfloat16),
        tokens_grad,
        query_weight_grad,
        query_bias_grad,
        key_weight_grad,
        value_weight_grad,
        value_bias_grad,
        out_weight_grad,
        out_bias_grad,
        first_gain_grad,
        first_shift_grad,
        up_weight_grad,
        up_bias_grad,
        down_weight_grad,
        down_bias_grad,
        second_gain_grad,
        second_shift_grad,
    )


MESH = pl.DeviceIdType.MESH
VMEM_BYTES = 63 * 1024 * 1024
CHUNKS = 4
KINDS = "HBHB"
MORE_X = "HHHB"
JOBS = len(KINDS)


def flip(index, bit):
    low = index // bit % 2
    return index + bit * (1 - 2 * low)


def mp_peer(relation):
    dp, mp = lax.axis_index("dp"), lax.axis_index("mp")
    for bit in (1, 2):
        if relation // bit % 2:
            mp = flip(mp, bit)
    return (dp, mp)


def dp_peer(bit):
    return (flip(lax.axis_index("dp"), bit), lax.axis_index("mp"))


def greet(peers):
    barrier = pltpu.get_barrier_semaphore()
    for device in peers:
        pl.semaphore_signal(barrier, inc=1, device_id=device, device_id_type=MESH)
    pl.semaphore_wait(barrier, len(peers))


def remote(src, dst, send, recv, device):
    return pltpu.make_async_remote_copy(
        src_ref=src, dst_ref=dst, send_sem=send, recv_sem=recv, device_id=device, device_id_type=MESH
    )


def repeat(count, body):
    def step(i, carry):
        body(i)
        return carry

    lax.fori_loop(0, count, step, 0)


class Gather:
    def __init__(self, land, send, recv, chunks=CHUNKS):
        self.land, self.send, self.recv, self.chunks = land, send, recv, chunks
        self.size = land.shape[1] // chunks

    def copy(self, relation, j):
        rows = pl.ds(pl.multiple_of(j * self.size, self.size), self.size)
        return remote(
            self.land.at[2 if relation == 3 else 0, rows],
            self.land.at[relation, rows],
            self.send.at[relation - 1, j],
            self.recv.at[relation - 1, j],
            mp_peer(2 if relation == 2 else 1),
        )

    def start(self, j):
        self.copy(2, j).start()
        self.copy(1, j).start()

    def arrive(self, relation, j):
        self.copy(relation, j).wait_recv()
        if relation == 2:
            self.copy(3, j).start()

    def drain(self):
        def body(j):
            for relation in (1, 2, 3):
                self.copy(relation, j).wait_send()

        repeat(self.chunks, body)


PAIR, FAR, NEAR = 0, 1, 2


class Reduce:
    def __init__(self, out, land, send, recv, chunks=CHUNKS):
        self.out, self.land, self.send, self.recv, self.chunks = out, land, send, recv, chunks
        self.size = out.shape[1] // chunks

    def copy(self, kind, j):
        rows = pl.ds(j * self.size, self.size)
        return remote(
            self.out.at[kind, rows],
            self.land.at[kind, rows],
            self.send.at[kind, j],
            self.recv.at[kind, j],
            mp_peer(2 if kind == FAR else 1),
        )

    def post(self, kind, j, value):
        self.out[kind, pl.ds(j * self.size, self.size)] = value.astype(BF)
        self.copy(kind, j).start()

    def forward_pair(self, j, mine):
        self.copy(PAIR, j).wait_recv()
        rows = pl.ds(j * self.size, self.size)
        self.post(FAR, j, mine + self.land[PAIR, rows].astype(F32))

    def total(self, j, mine):
        self.copy(NEAR, j).wait_recv()
        self.copy(FAR, j).wait_recv()
        rows = pl.ds(j * self.size, self.size)
        return mine + self.land[NEAR, rows].astype(F32) + self.land[FAR, rows].astype(F32)

    def drain(self):
        def body(j):
            for kind in (PAIR, FAR, NEAR):
                self.copy(kind, j).wait_send()

        repeat(self.chunks, body)


ROUTES = {"H": "xlh", "B": "lxh"}


class Spread:
    def __init__(self, data, full, land, send, recv, kinds, first=0, last=3):
        self.data, self.full, self.land, self.send, self.recv = data, full, land, send, recv
        self.sums, self.hands = first < 2, last > 1
        self.kinds, self.jobs = kinds, len(kinds)
        self.count = (full if data is None else data).shape[0] // self.jobs

    def route(self, job):
        return ROUTES[self.kinds[job if isinstance(job, int) else 0]]

    def side(self, axis):
        dp = lax.axis_index("dp")
        return {"x": dp % 2, "z": dp // 2, "l": dp // 2 % 2, "h": dp // 4}[axis]

    def range_of(self, start, size):
        return pl.ds(pl.multiple_of(start, size), size)

    def place(self, job, level):
        start, size = job * self.count, self.count
        for axis in self.route(job)[:level]:
            size //= 4 if axis == "z" else 2
            start += self.side(axis) * size
        return start, size

    def landing(self, job, stage, k=1):
        at, size = 0, self.count
        for level in range(stage + 1):
            ways = 4 if self.route(job)[level] == "z" else 2
            size //= ways
            if level < stage:
                at += size * (ways - 1)
        return self.land.at[job, pl.ds(at + (k - 1) * size, size)]

    def copies(self, job, stage):
        dp, mp = lax.axis_index("dp"), lax.axis_index("mp")
        levels = len(self.route(job))
        back = stage >= levels
        level = 2 * levels - 1 - stage if back else stage
        start, size = self.place(job, level)
        axis = self.route(job)[level]
        here = self.side(axis)
        ways, step = (4, 2) if axis == "z" else (2, {"x": 1, "l": 2, "h": 4}[axis])
        found = []
        for k in range(1, ways):
            there = (here + k) % ways
            if back:
                src = dst = self.full.at[self.range_of(*self.place(job, level + 1))]
            else:
                src = self.data.at[self.range_of(start + there * (size // ways), size // ways)]
                dst = self.landing(job, level, k)
            at = (job, stage * 3 + k - 1)
            device = (dp + (there - here) * step, mp)
            found.append(remote(src, dst, self.send.at[at], self.recv.at[at], device))
        return found

    def own(self, job):
        return self.range_of(*self.place(job, len(self.route(job))))

    def stages(self, job):
        levels = len(self.route(job))
        return (0 if self.sums else levels), (2 * levels if self.hands else levels)

    def step(self, job, stage):
        first, end = self.stages(job)
        levels = len(self.route(job))
        if stage > first:
            arrived = self.copies(job, stage - 1)
            for done in arrived:
                done.wait_send()
                done.wait_recv()
            if stage <= levels:
                rows = self.range_of(*self.place(job, stage))
                total = self.data[rows].astype(F32)
                for k in range(len(arrived)):
                    total += self.landing(job, stage - 1, k + 1)[...].astype(F32)
                target = self.full if stage == levels and self.full is not None else self.data
                target[rows] = total.astype(BF)
        if stage < end:
            for copy in self.copies(job, stage):
                copy.start()


def advance(*moves):
    for total, jobs, stage in moves:
        for job in jobs if isinstance(jobs, tuple) else (jobs,):
            total.step(job, stage)


def spread_land(data, kinds):
    count = data[0] // len(kinds)
    return pltpu.VMEM((len(kinds), count - count // 8, data[1]), BF)


def spread_sems(kinds):
    return [pltpu.SemaphoreType.DMA((len(kinds), 18)), pltpu.SemaphoreType.DMA((len(kinds), 18))]


class Hops:
    def __init__(self, value, land, send, recv, peers):
        self.value, self.land, self.send, self.recv, self.peers = value, land, send, recv, peers

    def copy(self, i):
        return remote(
            self.value.at[i], self.land.at[i], self.send.at[i], self.recv.at[i], self.peers[i]
        )

    def start(self, i):
        self.copy(i).start()

    def finish(self, i):
        self.copy(i).wait_recv()
        self.value[i + 1] = self.value[i] + self.land[i]
        self.copy(i).wait_send()


def hop_scratch(count, *shape):
    return [
        pltpu.VMEM((count + 1, *shape), F32),
        pltpu.VMEM((count, *shape), F32),
        pltpu.SemaphoreType.DMA((count,)),
        pltpu.SemaphoreType.DMA((count,)),
    ]


def greet_all():
    dp, mp = lax.axis_index("dp"), lax.axis_index("mp")
    across = [((dp // 2 + k) % 4 * 2 + dp % 2, mp) for k in (1, 2, 3)]
    greet([mp_peer(1), mp_peer(2), dp_peer(1), *across])


def transfer_sems(chunks=CHUNKS):
    return [pltpu.SemaphoreType.DMA((3, chunks)), pltpu.SemaphoreType.DMA((3, chunks))]


def comm_params(collective_id):
    return pltpu.CompilerParams(
        collective_id=collective_id, has_side_effects=True, vmem_limit_bytes=VMEM_BYTES
    )


WHOLE = pl.BlockSpec(memory_space=pltpu.VMEM)


def shaped(*shape, dtype=None):
    return jax.ShapeDtypeStruct(shape, dtype or BF)


def as_row(ref):
    return ref[...].astype(F32)[None]


def column_sum(value):
    return jnp.sum(value, 0, keepdims=True)


def row_mean(value):
    return jnp.mean(value, -1, keepdims=True)


def project_kernel(
    x_ref, wq_ref, wk_ref, wv_ref, qb_ref, vb_ref, q_ref, k_ref, v_ref, vt_ref, all_ref, land, send, recv, save
):
    rows_here = land.shape[1]
    load = pltpu.make_async_copy(x_ref, land.at[0], save.at[0])
    load.start()
    load.wait()
    greet([mp_peer(1), mp_peer(2)])
    gather = Gather(land, send, recv)
    repeat(CHUNKS, gather.start)
    size = gather.size

    def store(s, j):
        rows = pl.ds(pl.multiple_of(j * size, size), size)
        return pltpu.make_async_copy(land.at[s, rows], all_ref.at[s, rows], save.at[1 + s * CHUNKS + j])

    def emit(x, at):
        rows = pl.ds(pl.multiple_of(at, x.shape[0]), x.shape[0])
        q = (mm(x, wq_ref[...], 1, 0) + as_row(qb_ref)).astype(BF)
        q_ref[rows] = (q.astype(F32) * HD**-0.5).astype(BF)
        k_ref[rows] = mm(x, wk_ref[...], 1, 0).astype(BF)
        v = mm(x, wv_ref[...], 1, 0) + as_row(vb_ref)
        v_ref[rows] = v.astype(BF)
        vt_ref[:, rows] = v.T.astype(BF)

    def close(i):
        s, j = i // 2, i % 2 * 2

        @pl.when(i >= 2)
        def _():
            gather.arrive(1, j)
            gather.arrive(1, j + 1)

        emit(land[s, pl.ds(pl.multiple_of(j * size, 2 * size), 2 * size)], i * 2 * size)
        store(s, j).start()
        store(s, j + 1).start()

    repeat(4, close)

    def far(j):
        gather.arrive(2, j)
        gather.arrive(3, j)

        def one(k):
            emit(land[2 + k, pl.ds(pl.multiple_of(j * size, size), size)], (2 + k) * rows_here + j * size)
            store(2 + k, j).start()

        repeat(2, one)

    repeat(CHUNKS, far)
    gather.drain()
    repeat(4, lambda s: repeat(CHUNKS, lambda j: store(s, j).wait()))


def gather_project(tokens, wq, wk, wv, q_bias, v_bias):
    rows, width = tokens.shape
    cols = wq.shape[1]
    return pl.pallas_call(
        project_kernel,
        in_specs=[pl.BlockSpec(memory_space=pl.ANY)] + [WHOLE] * 5,
        out_specs=[WHOLE] * 4 + [pl.BlockSpec(memory_space=pl.ANY)],
        out_shape=[shaped(4 * rows, cols)] * 3 + [shaped(cols, 4 * rows), shaped(4, rows, width)],
        scratch_shapes=[
            pltpu.VMEM((4, rows, width), BF),
            *transfer_sems(),
            pltpu.SemaphoreType.DMA((4 * CHUNKS + 1,)),
        ],
        name="gather_project",
        compiler_params=comm_params(0),
    )(tokens, wq, wk, wv, q_bias, v_bias)


HALVES = 2


def forward_order(step):
    far = 2 * (3 - step % 2) + step // 2
    near = 2 * (1 - (step - 4) // 2) + step % 2
    return jnp.where(step < 4, far, near)


def attend_kernel(
    len_ref, q_ref, k_ref, vt_ref, w_ref, x_ref, ob_ref, gain_ref, shift_ref,
    e_ref, o_ref, r_ref, n_ref, i_ref, h_ref,
    k_aug, v_aug, out, land, mine, pending, send, recv,
):
    step = pl.program_id(0)
    seq_len, block = k_ref.shape[0], q_ref.shape[0]
    pairs = k_ref.shape[1] // WIDE
    reduce = Reduce(out, land, send, recv, HALVES)

    @pl.when(step == 0)
    def _():
        greet([mp_peer(1), mp_peer(2)])
        lanes = lax.broadcasted_iota(jnp.int32, (seq_len, WIDE), 1)
        rows = lax.broadcasted_iota(jnp.int32, (x_ref.shape[0], WIDE), 0)
        bias = jnp.concatenate(
            [
                jnp.where(rows + mp_peer(s)[1] * x_ref.shape[0] < len_ref[0, 0], 0.0, MASKED)
                for s in range(4)
            ],
            0,
        )
        for p in range(pairs):
            keys = k_ref[:, p * WIDE : (p + 1) * WIDE].astype(F32)
            for h in range(2):
                other = (1 - h) * HD
                k_aug[2 * p + h] = jnp.where(
                    lanes // HD == h, keys, jnp.where(lanes == other, bias, 0.0)
                ).astype(BF)
                at = (2 * p + h) * HD
                v_aug[2 * p + h, :HD] = vt_ref[at : at + HD, :]
                v_aug[2 * p + h, HD:] = jnp.ones((16, seq_len), BF)

    lanes = lax.broadcasted_iota(jnp.int32, (block, WIDE), 1)
    outs = []
    for p in range(pairs):
        query = q_ref[:, p * WIDE : (p + 1) * WIDE].astype(F32)
        scores = []
        for h in range(2):
            other = (1 - h) * HD
            q_aug = jnp.where(
                lanes // HD == h, query, jnp.where(lanes == other, 1.0, 0.0)
            ).astype(BF)
            scores.append(mm(k_aug[2 * p + h], q_aug, 1, 1))
        for h in range(2):
            top = jnp.max(scores[h], 0, keepdims=True)
            expon = jnp.exp(scores[h] - top).astype(BF)
            e_ref[0, 2 * p + h] = expon
            total = mm(v_aug[2 * p + h], expon, 1, 0)
            inverse = 1.0 / total[HD : HD + 1]
            r_ref[0, 2 * p + h] = inverse
            outs.append(total[:HD] * inverse)
    attended = jnp.concatenate(outs, 0).T.astype(BF)
    o_ref[...] = attended
    partial_rows = mm(attended, w_ref[...], 1, 0)

    for t in range(4 * HALVES):

        @pl.when(step == t)
        def _(t=t):
            if t < 4 and t % 2 == 0:
                reduce.post(PAIR, t // 2, partial_rows)
            elif t < 4:
                pending[...] = partial_rows
                reduce.forward_pair(t // 2, pending[...])
            elif t < 6:
                reduce.post(NEAR, t - 4, partial_rows)
            else:
                mine[pl.ds((t - 6) * block, block)] = partial_rows

    @pl.when(step == 4 * HALVES - 1)
    def _():
        for j in range(HALVES):
            rows = pl.ds(j * block, block)
            resid = x_ref[rows].astype(F32) + reduce.total(j, mine[rows]) + as_row(ob_ref)
            center = resid - row_mean(resid)
            inv_std = lax.rsqrt(row_mean(center * center) + epsilon)
            normed = center * inv_std
            n_ref[rows] = normed
            i_ref[rows] = inv_std
            h_ref[rows] = (normed * as_row(gain_ref) + as_row(shift_ref)).astype(BF)
        reduce.drain()


def attend(lengths, q, k, vt, out_weight, tokens, *vectors):
    all_rows, cols = q.shape
    rows, width = tokens.shape
    block = rows // HALVES
    heads = cols // HD
    steps = all_rows // block

    def fixed(*shape):
        return pl.BlockSpec(shape, lambda i: (0,) * len(shape))

    return pl.pallas_call(
        attend_kernel,
        grid=(steps,),
        in_specs=[
            pl.BlockSpec(memory_space=pltpu.SMEM),
            pl.BlockSpec((block, cols), lambda i: (forward_order(i), 0)),
            fixed(all_rows, cols),
            fixed(cols, all_rows),
            fixed(cols, width),
            fixed(rows, width),
            *[fixed(width)] * 3,
        ],
        out_specs=[
            pl.BlockSpec((1, heads, all_rows, block), lambda i: (forward_order(i), 0, 0, 0)),
            pl.BlockSpec((block, cols), lambda i: (forward_order(i), 0)),
            pl.BlockSpec((1, heads, 1, block), lambda i: (forward_order(i), 0, 0, 0)),
            fixed(rows, width),
            fixed(rows, 1),
            fixed(rows, width),
        ],
        out_shape=[
            shaped(steps, heads, all_rows, block),
            shaped(all_rows, cols),
            shaped(steps, heads, 1, block, dtype=F32),
            shaped(rows, width, dtype=F32),
            shaped(rows, 1, dtype=F32),
            shaped(rows, width),
        ],
        scratch_shapes=[
            pltpu.VMEM((heads, all_rows, WIDE), BF),
            pltpu.VMEM((heads, HD + 16, all_rows), BF),
            pltpu.VMEM((3, rows, width), BF),
            pltpu.VMEM((3, rows, width), BF),
            pltpu.VMEM((rows, width), F32),
            pltpu.VMEM((block, width), F32),
            *transfer_sems(HALVES),
        ],
        name="attend",
        compiler_params=comm_params(1),
    )(lengths, q, k, vt, out_weight, tokens, *vectors)


ROOT_HALF = 0.7071067811865476
ROOT_TAU = 0.3989422804014327


def feed_forward_kernel(
    h_ref, n_ref, i_ref, g_ref, up_ref, ub_ref, down_ref, *refs
):
    vectors, refs = refs[:5], refs[5:]
    (
        out_ref, b1_ref, r1_ref, upg_ref, downg_ref, small_ref,
        hidden, act, slope, branch, out1, land1, out2, land2, mine, pending, r2,
        gs1, gr1, gs2, gr2, rs1, rr1, rs2, rr2,
        down_land, down_send, down_recv, load,
    ) = refs
    rows_here, width = h_ref.shape
    fetch = pltpu.make_async_copy(h_ref, hidden.at[0], load.at[0])
    fetch.start()
    size = rows_here // CHUNKS
    first_gain, first_shift, down_bias, second_gain, second_shift = map(as_row, vectors)
    greet_all()
    down_sum = Spread(downg_ref, None, down_land, down_send, down_recv, KINDS, 0, 1)
    gather1, gather2 = Gather(hidden, gs1, gr1), Gather(branch, gs2, gr2)
    reduce1, reduce2 = Reduce(out1, land1, rs1, rr1), Reduce(out2, land2, rs2, rr2)
    fetch.wait()
    repeat(CHUNKS, gather1.start)
    small_ref[...] = jnp.zeros_like(small_ref)

    def forward(x):
        pre = mm(x, up_ref[...], 1, 0) + as_row(ub_ref)
        cdf = 0.5 + 0.5 * lax.erf(pre * ROOT_HALF)
        active = (pre * cdf).astype(BF)
        steep = (cdf + pre * jnp.exp(-0.5 * pre * pre) * ROOT_TAU).astype(BF)
        return active, steep, mm(active, down_ref[...], 1, 0)

    def backward(grad, steep):
        pre_grad = (mm(grad, down_ref[...], 1, 1) * steep.astype(F32)).astype(BF)
        small_ref[6:7] += column_sum(pre_grad.astype(F32))
        return pre_grad, mm(pre_grad, up_ref[...], 1, 1)

    def chunk_rows(j):
        return pl.ds(pl.multiple_of(j * size, size), size)

    def double_rows(j):
        return pl.ds(pl.multiple_of(j * 2 * size, 2 * size), 2 * size)

    def halves(value):
        return value[:size], value[size:]

    def close_forward(i):
        s, half = i // 2, i % 2
        rows = double_rows(half)

        @pl.when(i >= 2)
        def _():
            gather1.arrive(1, 2 * half)
            gather1.arrive(1, 2 * half + 1)

        act[s, rows], slope[s, rows], part = forward(hidden[s, rows])

        @pl.when(i < 2)
        def _():
            mine[rows] = part

        @pl.when(i >= 2)
        def _():
            for k, piece in enumerate(halves(part)):
                reduce1.post(NEAR, 2 * half + k, piece)

    def far_forward(j):
        gather1.arrive(2, j)
        gather1.arrive(3, j)
        rows = chunk_rows(j)
        active, steep, part = forward(jnp.concatenate([hidden[2, rows], hidden[3, rows]], 0))
        for s in (2, 3):
            act[s, rows] = halves(active)[s - 2]
            slope[s, rows] = halves(steep)[s - 2]
        pending[rows] = part[:size]
        reduce1.post(PAIR, j, part[size:])

        @pl.when(j > 0)
        def _():
            reduce1.forward_pair(j - 1, pending[chunk_rows(j - 1)])

    repeat(4, close_forward)
    repeat(CHUNKS, far_forward)
    reduce1.forward_pair(CHUNKS - 1, pending[chunk_rows(CHUNKS - 1)])

    def second_norm(j):
        rows = chunk_rows(j)
        hidden = n_ref[rows] * first_gain + first_shift
        resid = hidden + reduce1.total(j, mine[rows]) + down_bias
        center = resid - row_mean(resid)
        inv_std = lax.rsqrt(row_mean(center * center) + epsilon)
        normed = center * inv_std
        out_ref[rows] = (normed * second_gain + second_shift).astype(BF)
        grad = g_ref[rows].astype(F32)
        product = grad * normed
        small_ref[0:1] += column_sum(product)
        small_ref[1:2] += column_sum(grad)
        scaled = grad * second_gain
        back = inv_std * (scaled - row_mean(scaled) - normed * row_mean(scaled * normed))
        small_ref[2:3] += column_sum(back)
        r2[rows] = back
        branch[0, rows] = back.astype(BF)
        gather2.start(j)

    repeat(CHUNKS, second_norm)

    def close_backward(i):
        s, half = i // 2, i % 2
        rows = double_rows(half)

        @pl.when(i >= 2)
        def _():
            gather2.arrive(1, 2 * half)
            gather2.arrive(1, 2 * half + 1)

        slope[s, rows], part = backward(branch[s, rows], slope[s, rows])

        @pl.when(i < 2)
        def _():
            mine[rows] = part

        @pl.when(i >= 2)
        def _():
            for k, piece in enumerate(halves(part)):
                reduce2.post(NEAR, 2 * half + k, piece)

    def far_backward(j):
        gather2.arrive(2, j)
        gather2.arrive(3, j)
        rows = chunk_rows(j)
        pre_grad, part = backward(
            jnp.concatenate([branch[2, rows], branch[3, rows]], 0),
            jnp.concatenate([slope[2, rows], slope[3, rows]], 0),
        )
        for s in (2, 3):
            slope[s, rows] = halves(pre_grad)[s - 2]
        pending[rows] = part[:size]
        reduce2.post(PAIR, j, part[size:])

        @pl.when(j > 0)
        def _():
            reduce2.forward_pair(j - 1, pending[chunk_rows(j - 1)])

    repeat(4, close_backward)
    repeat(CHUNKS, far_backward)
    reduce2.forward_pair(CHUNKS - 1, pending[chunk_rows(CHUNKS - 1)])

    tile = 256

    def down_grad(t):
        cols = pl.ds(pl.multiple_of(t * tile, tile), tile)
        total = mm(act[0, :, cols], branch[0], 0, 0)
        for s in (1, 2, 3):
            total += mm(act[s, :, cols], branch[s], 0, 0)
        downg_ref[cols] = total.astype(BF)

    def up_grad(t):
        cols = pl.ds(pl.multiple_of(t * tile, tile), tile)
        total = mm(hidden[0, :, cols], slope[0], 0, 0)
        for s in (1, 2, 3):
            total += mm(hidden[s, :, cols], slope[s], 0, 0)
        upg_ref[cols] = total.astype(BF)

    repeat(2, down_grad)
    advance((down_sum, (0, 1), 0))
    repeat(2, lambda t: down_grad(t + 2))
    advance((down_sum, (2, 3), 0))
    repeat(width // tile, up_grad)

    def first_norm(j):
        rows = chunk_rows(j)
        normed = n_ref[rows]
        grad = r2[rows] + reduce2.total(j, mine[rows])
        small_ref[3:4] += column_sum(grad * normed)
        small_ref[4:5] += column_sum(grad)
        scaled = grad * first_gain
        back = i_ref[rows] * (scaled - row_mean(scaled) - normed * row_mean(scaled * normed))
        small_ref[5:6] += column_sum(back)
        r1_ref[rows] = back
        b1_ref[rows] = back.astype(BF)

    advance((down_sum, (0, 1), 1))
    first_norm(0)
    advance((down_sum, (2, 3), 1))
    first_norm(1)
    advance((down_sum, (0, 1), 2))
    first_norm(2)
    advance((down_sum, (2, 3), 2))
    first_norm(3)
    advance((down_sum, (0, 1, 2, 3), 3))
    for transfer in (gather1, gather2, reduce1, reduce2):
        transfer.drain()


def feed_forward(hidden, normed, inv_std, output_grad, up, up_bias, down, *vectors):
    rows, width = hidden.shape
    units = up.shape[1]
    tall = (4, rows, units)
    return pl.pallas_call(
        feed_forward_kernel,
        in_specs=[pl.BlockSpec(memory_space=pl.ANY)] + [WHOLE] * 11,
        out_specs=[WHOLE] * 6,
        out_shape=[
            shaped(rows, width),
            shaped(rows, width),
            shaped(rows, width, dtype=F32),
            shaped(width, units),
            shaped(units, width),
            shaped(8, width, dtype=F32),
        ],
        scratch_shapes=[
            pltpu.VMEM((4, rows, width), BF),
            pltpu.VMEM(tall, BF),
            pltpu.VMEM(tall, BF),
            pltpu.VMEM((4, rows, width), BF),
            *[pltpu.VMEM((3, rows, width), BF)] * 4,
            *[pltpu.VMEM((rows, width), F32)] * 3,
            *transfer_sems(),
            *transfer_sems(),
            *transfer_sems(),
            *transfer_sems(),
            spread_land((units, width), KINDS),
            *spread_sems(KINDS),
            pltpu.SemaphoreType.DMA((1,)),
        ],
        name="feed_forward",
        compiler_params=comm_params(2),
    )(hidden, normed, inv_std, output_grad, up, up_bias, down, *vectors)


def attend_back_kernel(
    b_ref, w_ref, e_ref, r_ref, q_ref, k_ref, v_ref, o_ref, small_in, up_in, down_in, all_in,
    dq_ref, dk_ref, dv_ref, wg_ref, pg_ref, small_ref, up_out, down_out,
    land, v_aug, k_t, dks, dvs, dqs, w_total, w_low, p_low, grads, up, down, tokens, loads, send, recv,
    up_land, up_send, up_recv, down_send, down_recv, out_land, out_send, out_recv,
    pair_land, pair_send, pair_recv, value, small_land, small_send, small_recv,
):
    step = pl.program_id(0)
    pair, s_now = step // 2 % 2, step // 4 * 2 + step % 2
    seq_len, block = k_ref.shape[0], q_ref.shape[0]
    pieces = e_ref.shape[0]
    cols = w_ref.shape[0]
    width = w_ref.shape[1]
    half = block // 2
    gather = Gather(land, send, recv, HALVES)
    up_sum = Spread(up, None, up_land, up_send, up_recv, MORE_X, 0, 1)
    down_sum = Spread(None, down, None, down_send, down_recv, KINDS, 2, 3)
    out_sum = Spread(w_low, None, out_land, out_send, out_recv, "H", 0, 1)
    pair_sum = Spread(p_low, None, pair_land, pair_send, pair_recv, MORE_X, 0, 1)
    small = Hops(
        value, small_land, small_send, small_recv,
        [dp_peer(1), dp_peer(2), dp_peer(4), mp_peer(1), mp_peer(2)],
    )
    load_up = pltpu.make_async_copy(up_in, up, loads.at[0])
    load_down = [
        pltpu.make_async_copy(
            down_in.at[down_sum.own(job)], down.at[down_sum.own(job)], loads.at[5 + job]
        )
        for job in range(JOBS)
    ]
    load_tokens = pltpu.make_async_copy(all_in, tokens, loads.at[2])
    save_up = pltpu.make_async_copy(up, up_out, loads.at[3])
    save_down = pltpu.make_async_copy(down, down_out, loads.at[4])

    load_branch = pltpu.make_async_copy(b_ref, land.at[0], loads.at[5 + JOBS])

    @pl.when(step == 0)
    def _():
        load_branch.start()
        for load in load_down:
            load.start()
        load_up.start()
        load_tokens.start()
        value[0] = small_in[...]
        w_total[...] = jnp.zeros_like(w_total)
        greet_all()
        small.start(0)
        load_branch.wait()
        repeat(HALVES, gather.start)
        for load in load_down:
            load.wait()
        advance((down_sum, (0, 1, 2, 3), 3))
        load_up.wait()
        advance((up_sum, (3, 0, 1, 2), 0))

    @pl.when(step == 1)
    def _():
        repeat(HALVES, lambda j: gather.arrive(1, j))

    @pl.when(step == 2)
    def _():
        small.finish(0)
        small.start(1)
        advance((down_sum, (0, 1, 2, 3), 4), (up_sum, (3, 0), 1))

    @pl.when(step == 3)
    def _():
        advance((up_sum, (1, 2), 1), (down_sum, (0, 1), 5))

    @pl.when(step == 4)
    def _():
        small.finish(1)
        small.start(2)
        advance((up_sum, (3, 0), 2), (down_sum, (2, 3), 5))
        repeat(HALVES, lambda j: gather.arrive(2, j))

    @pl.when(step == 5)
    def _():
        repeat(HALVES, lambda j: gather.arrive(3, j))

    @pl.when(pair == 0)
    def _():
        branch = land[s_now]
        w_total[...] += mm(o_ref[...], branch, 0, 0)
        grads[pl.ds(pl.multiple_of(s_now * block, block), block)] = mm(
            branch, w_ref[...], 1, 1
        ).astype(BF)

    @pl.when(step == 5)
    def _():
        w_low[...] = w_total[...].astype(BF)
        advance((out_sum, 0, 0), (up_sum, (1, 2), 2))

    @pl.when(step == 6)
    def _():
        small.finish(2)
        small.start(3)
        advance((out_sum, 0, 1), (up_sum, (3, 0), 3), (down_sum, (0, 1), 6))

    @pl.when(step == 7)
    def _():
        small.finish(3)
        small.start(4)
        advance(
            (pair_sum, (3, 0, 1, 2), 1), (out_sum, 0, 2), (up_sum, (1, 2), 3), (down_sum, (2, 3), 6)
        )
        save_up.start()
        save_down.start()

    @pl.when(s_now == 0)
    def _():
        lanes = lax.broadcasted_iota(jnp.int32, (seq_len, WIDE), 1)
        values = v_ref[...].astype(F32)
        for h in range(2):
            other = (1 - h) * HD
            ones = jnp.where((lanes >= other) & (lanes < other + 2), 1.0, 0.0)
            v_aug[pair, h] = jnp.where(lanes // HD == h, values, ones).astype(BF)
        k_t[pair] = (k_ref[...].astype(F32) * HD**-0.5).T.astype(BF)
        dks[pair] = jnp.zeros(dks.shape[1:], F32)
        dvs[pair] = jnp.zeros(dvs.shape[1:], F32)

    lanes = lax.broadcasted_iota(jnp.int32, (block, WIDE), 1)
    row_start = pl.multiple_of(s_now * block, block)
    inverse = jnp.concatenate(
        [
            jnp.concatenate(
                [jnp.broadcast_to(r_ref[i, h], (HD, block // pieces)) for h in range(2)], 0
            )
            for i in range(pieces)
        ],
        1,
    ).T
    wide = pl.ds(pl.multiple_of(pair * WIDE, WIDE), WIDE)
    grad = (grads[pl.ds(row_start, block), wide].astype(F32) * inverse).astype(BF)
    grad_wide = grad.astype(F32)
    product = grad_wide * o_ref[:, wide].astype(F32)
    centered = []
    for h in range(2):
        other = (1 - h) * HD
        inside = lanes // HD == h
        row_dot = jnp.sum(jnp.where(inside, product, 0.0), -1, keepdims=True)
        high = row_dot.astype(BF).astype(F32)
        g_aug = jnp.where(
            inside,
            grad_wide,
            jnp.where(lanes == other, -high, jnp.where(lanes == other + 1, high - row_dot, 0.0)),
        ).astype(BF)
        centered.append(mm(v_aug[pair, h], g_aug, 1, 1))
    query_grads = []
    for h in range(2):
        cols_h = slice(h * HD, (h + 1) * HD)
        expon = jnp.concatenate([e_ref[i, h] for i in range(pieces)], 1)
        score_grad = (expon.astype(F32) * centered[h]).astype(BF)
        dvs[pair, h] += mm(expon, grad[:, cols_h], 1, 0)
        dks[pair, h] += mm(score_grad, q_ref[:, cols_h], 1, 0)
        query_grads.append(mm(k_t[pair, cols_h, :], score_grad, 1, 0))
    query_grad = jnp.concatenate(query_grads, 0).T.astype(BF)
    dq_ref[...] = query_grad
    dqs[pair, pl.ds(row_start, block), :WIDE] = query_grad

    @pl.when(s_now == 3)
    def _():
        for total, out, at in ((dks, dk_ref, WIDE), (dvs, dv_ref, 2 * WIDE)):
            joined = jnp.concatenate([total[pair, h] for h in range(2)], 1).astype(BF)
            out[:, wide] = joined
            dqs[pair, :, at : at + WIDE] = joined

    @pl.when(step == 5)
    def _():
        load_tokens.wait()
        projection_grads(tokens, dqs.at[0], p_low)
        advance((pair_sum, (3, 0, 1, 2), 0))

    @pl.when(step == 7)
    def _():
        advance((pair_sum, (3, 0, 1, 2), 2), (out_sum, 0, 3), (pair_sum, (3, 0, 1, 2), 3))
        small.finish(4)
        small_ref[...] = value[5]
        small_ref[6:7] = value[3, 6:7]
        wg_ref[...] = w_low[...]
        pg_ref[...] = p_low[...]
        gather.drain()
        save_down.wait()
        save_up.wait()


def projection_grads(tokens, joint, out_ref):
    tile = 256
    rows = tokens.shape[1]

    def body(t):
        cols = pl.ds(pl.multiple_of(t * tile, tile), tile)
        total = mm(tokens[0, :, cols], joint[pl.ds(0, rows)], 0, 0)
        for s in (1, 2, 3):
            total += mm(tokens[s, :, cols], joint[pl.ds(s * rows, rows)], 0, 0)
        out_ref[cols] = total.astype(BF)

    repeat(tokens.shape[2] // tile, body)


def attend_back(branch, out_weight, expon, inverse, q, k, v, attended, small, up, down, gathered):
    rows, width = branch.shape
    all_rows, cols = q.shape
    pairs = cols // WIDE
    pieces = HALVES

    def fixed(*shape):
        return pl.BlockSpec(shape, lambda i: (0,) * len(shape))

    def pair_at(i):
        return i // 2 % 2

    def rows_at(i):
        return i // 4 * 2 + i % 2

    anywhere = pl.BlockSpec(memory_space=pl.ANY)
    pair_rows = pl.BlockSpec((rows, WIDE), lambda i: (rows_at(i), pair_at(i)))
    pair_keys = pl.BlockSpec((all_rows, WIDE), lambda i: (0, pair_at(i)))
    return pl.pallas_call(
        attend_back_kernel,
        grid=(4 * pairs,),
        in_specs=[
            anywhere,
            fixed(cols, width),
            pl.BlockSpec((pieces, 2, all_rows, rows // pieces), lambda i: (rows_at(i), pair_at(i), 0, 0)),
            pl.BlockSpec((pieces, 2, 1, rows // pieces), lambda i: (rows_at(i), pair_at(i), 0, 0)),
            pair_rows,
            pair_keys,
            pair_keys,
            pl.BlockSpec((rows, cols), lambda i: (rows_at(i), 0)),
            fixed(*small.shape),
            anywhere,
            anywhere,
            anywhere,
        ],
        out_specs=[
            pair_rows,
            fixed(all_rows, cols),
            fixed(all_rows, cols),
            fixed(cols, width),
            fixed(width, 3 * WIDE),
            fixed(*small.shape),
            anywhere,
            anywhere,
        ],
        out_shape=[shaped(all_rows, cols)] * 3
        + [
            shaped(cols, width),
            shaped(width, 3 * WIDE),
            shaped(*small.shape, dtype=F32),
            shaped(*up.shape),
            shaped(*down.shape),
        ],
        scratch_shapes=[
            pltpu.VMEM((4, rows, width), BF),
            pltpu.VMEM((pairs, 2, all_rows, WIDE), BF),
            pltpu.VMEM((pairs, WIDE, all_rows), BF),
            pltpu.VMEM((pairs, 2, all_rows, HD), F32),
            pltpu.VMEM((pairs, 2, all_rows, HD), F32),
            pltpu.VMEM((pairs, all_rows, 3 * WIDE), BF),
            pltpu.VMEM((cols, width), F32),
            pltpu.VMEM((cols, width), BF),
            pltpu.VMEM((width, 3 * WIDE), BF),
            pltpu.VMEM((all_rows, cols), BF),
            pltpu.VMEM(up.shape, BF),
            pltpu.VMEM(down.shape, BF),
            pltpu.VMEM(gathered.shape, BF),
            pltpu.SemaphoreType.DMA((6 + JOBS,)),
            *transfer_sems(HALVES),
            spread_land(up.shape, MORE_X),
            *spread_sems(KINDS),
            *spread_sems(KINDS),
            spread_land((cols, width), "H"),
            *spread_sems("H"),
            spread_land((width, 3 * WIDE), KINDS),
            *spread_sems(KINDS),
            *hop_scratch(5, *small.shape),
        ],
        name="attend_back",
        compiler_params=comm_params(3),
    )(branch, out_weight, expon, inverse, q, k, v, attended, small, up, down, gathered)


def input_back_kernel(
    dq_ref, dk_ref, dv_ref, wq_ref, wk_ref, wv_ref, all_ref, r1_ref, wg_in, pg_in, up_in,
    x_ref, wg_ref, pg_ref, last_ref, bias_ref, up_out,
    out, land, mine, pending, send, recv, up, loads, up_send, up_recv, out_send, out_recv,
    pair_send, pair_recv, joint, w_full, p_full, last_full, last_low, last_land, last_send, last_recv,
    value, bias_land, bias_send, bias_recv,
):
    rows_here = r1_ref.shape[0]
    size = rows_here // CHUNKS
    last = dq_ref.shape[1] - WIDE
    up_sum = Spread(None, up, None, up_send, up_recv, MORE_X, 2, 3)
    out_sum = Spread(None, w_full, None, out_send, out_recv, "H", 2, 3)
    pair_sum = Spread(None, p_full, None, pair_send, pair_recv, MORE_X, 2, 3)
    last_sum = Spread(last_low, last_full, last_land, last_send, last_recv, KINDS)
    bias = Hops(value, bias_land, bias_send, bias_recv, [dp_peer(1), dp_peer(2), dp_peer(4)])
    reduce = Reduce(out, land, send, recv)
    save_up = pltpu.make_async_copy(up, up_out, loads.at[JOBS])
    load_up = [
        pltpu.make_async_copy(up_in.at[up_sum.own(job)], up.at[up_sum.own(job)], loads.at[job])
        for job in range(JOBS)
    ]
    for load in load_up:
        load.start()
    w_full[out_sum.own(0)] = wg_in[out_sum.own(0)]
    for job in range(JOBS):
        p_full[pair_sum.own(job)] = pg_in[pair_sum.own(job)]
    value[0, 0:1] = column_sum(dq_ref[...].astype(F32))
    value[0, 1:8] = jnp.broadcast_to(column_sum(dv_ref[...].astype(F32)), (7, dv_ref.shape[1]))
    greet_all()
    bias.start(0)
    for load in load_up:
        load.wait()
    advance((pair_sum, (3, 0, 1, 2), 3), (out_sum, 0, 3), (up_sum, (0, 1, 2, 3), 3))
    tail = pl.ds(last, WIDE)
    for at, grad in enumerate((dq_ref, dk_ref, dv_ref)):
        joint[:, at * WIDE : (at + 1) * WIDE] = grad[:, tail]
    projection_grads(all_ref, joint, last_low)
    advance((last_sum, (0, 1, 2, 3), 0))
    grads = ((dq_ref, wq_ref), (dk_ref, wk_ref), (dv_ref, wv_ref))

    def part_of(starts, count):
        total = None
        for grad, weight in grads:
            pieces = [grad[pl.ds(pl.multiple_of(at, size), count)] for at in starts]
            x = pieces[0] if len(pieces) == 1 else jnp.concatenate(pieces, 0)
            term = mm(x, weight[...], 1, 1)
            total = term if total is None else total + term
        return total

    def chunk_rows(j):
        return pl.ds(pl.multiple_of(j * size, size), size)

    def far(j):
        part = part_of((2 * rows_here + j * size, 3 * rows_here + j * size), size)
        pending[chunk_rows(j)] = part[:size]
        reduce.post(PAIR, j, part[size:])

        @pl.when(j > 0)
        def _():
            reduce.forward_pair(j - 1, pending[chunk_rows(j - 1)])

    repeat(CHUNKS, far)
    reduce.forward_pair(CHUNKS - 1, pending[chunk_rows(CHUNKS - 1)])
    bias.finish(0)
    bias.start(1)
    advance((pair_sum, (3, 0, 1, 2), 4), (last_sum, (0, 1, 2, 3), 1), (up_sum, (3, 0), 4))

    def near(i):
        part = part_of((rows_here + i * 2 * size,), 2 * size)
        reduce.post(NEAR, 2 * i, part[:size])
        reduce.post(NEAR, 2 * i + 1, part[size:])

    repeat(2, near)

    def own(i):
        mine[pl.ds(pl.multiple_of(i * 2 * size, 2 * size), 2 * size)] = part_of((i * 2 * size,), 2 * size)

    repeat(2, own)

    def finish(j):
        rows = chunk_rows(j)
        x_ref[rows] = (r1_ref[rows] + reduce.total(j, mine[rows])).astype(BF)

    advance((pair_sum, (3, 0, 1, 2), 5), (up_sum, (1, 2), 4))
    finish(0)
    bias.finish(1)
    bias.start(2)
    advance((last_sum, (0, 1, 2, 3), 2), (up_sum, (3, 0), 5), (out_sum, 0, 4))
    finish(1)
    advance((last_sum, (0, 1, 2, 3), 3), (up_sum, (1, 2), 5), (out_sum, 0, 5))
    finish(2)
    advance((last_sum, (0, 1, 2, 3), 4))
    finish(3)
    bias.finish(2)
    bias_ref[...] = value[3]
    advance((last_sum, (0, 1, 2, 3), 5), (up_sum, (0, 1, 2, 3), 6))
    save_up.start()
    advance((pair_sum, (3, 0, 1, 2), 6), (out_sum, 0, 6))
    wg_ref[...] = w_full[...]
    pg_ref[...] = p_full[...]
    advance((last_sum, (0, 1, 2, 3), 6))
    last_ref[...] = last_full[...]
    reduce.drain()
    save_up.wait()


def input_back(dq, dk, dv, wq, wk, wv, gathered, resid_grad, out_grad, pair_grad, up):
    rows, width = resid_grad.shape
    cols = dq.shape[1]
    return pl.pallas_call(
        input_back_kernel,
        in_specs=[WHOLE] * 10 + [pl.BlockSpec(memory_space=pl.ANY)],
        out_specs=[WHOLE] * 5 + [pl.BlockSpec(memory_space=pl.ANY)],
        out_shape=[
            shaped(rows, width),
            shaped(*out_grad.shape),
            shaped(*pair_grad.shape),
            shaped(*pair_grad.shape),
            shaped(8, cols, dtype=F32),
            shaped(*up.shape),
        ],
        scratch_shapes=[
            pltpu.VMEM((3, rows, width), BF),
            pltpu.VMEM((3, rows, width), BF),
            pltpu.VMEM((rows, width), F32),
            pltpu.VMEM((rows, width), F32),
            *transfer_sems(),
            pltpu.VMEM(up.shape, BF),
            pltpu.SemaphoreType.DMA((JOBS + 1,)),
            *spread_sems(KINDS),
            *spread_sems("H"),
            *spread_sems(KINDS),
            pltpu.VMEM((dq.shape[0], 3 * WIDE), BF),
            pltpu.VMEM(out_grad.shape, BF),
            *[pltpu.VMEM(pair_grad.shape, BF)] * 3,
            spread_land(pair_grad.shape, KINDS),
            *spread_sems(KINDS),
            *hop_scratch(3, 8, cols),
        ],
        name="input_back",
        compiler_params=comm_params(4),
    )(dq, dk, dv, wq, wk, wv, gathered, resid_grad, out_grad, pair_grad, up)


def widen_kernel(up_ref, down_ref, out_ref, pair_ref, last_ref, upw, downw, outw, qw, kw, vw):
    upw[...] = up_ref[...].astype(F32)
    downw[...] = down_ref[...].astype(F32)
    outw[...] = out_ref[...].astype(F32)
    for at, wide in enumerate((qw, kw, vw)):
        cols = slice(at * WIDE, (at + 1) * WIDE)
        wide[:, :WIDE] = pair_ref[:, cols].astype(F32)
        wide[:, WIDE:] = last_ref[:, cols].astype(F32)


def widen_grads(*grads):
    steps = 8
    shapes = [g.shape for g in grads[:3]] + [(grads[3].shape[0], 2 * WIDE)] * 3

    def tiles(shape):
        return pl.BlockSpec((shape[0] // steps, shape[1]), lambda i: (i, 0))

    return pl.pallas_call(
        widen_kernel,
        grid=(steps,),
        in_specs=[tiles(g.shape) for g in grads],
        out_specs=[tiles(shape) for shape in shapes],
        out_shape=[shaped(*shape, dtype=F32) for shape in shapes],
        name="widen_grads",
    )(*grads)


def per_device(
    tokens, lengths, query_weight, query_bias, key_weight, value_weight, value_bias, out_weight,
    out_bias, first_gain, first_shift, up_weight, up_bias, down_weight, down_bias, second_gain,
    second_shift, output_grad,
):
    pairs = query_weight.shape[1] // WIDE
    if (lax.axis_size("dp"), lax.axis_size("mp"), lengths.shape[1], pairs) != (8, 4, 1, 2):
        return per_device_general(
            tokens, lengths, query_weight, query_bias, key_weight, value_weight, value_bias,
            out_weight, out_bias, first_gain, first_shift, up_weight, up_bias, down_weight,
            down_bias, second_gain, second_shift, output_grad,
        )
    q, k, v, vt, gathered = gather_project(
        tokens, query_weight, key_weight, value_weight, query_bias, value_bias
    )
    expon, attended, inverse, normed, inv_std, hidden = attend(
        lengths, q, k, vt, out_weight, tokens, out_bias, first_gain, first_shift
    )
    layer_out, branch, resid_grad, up_grad, down_grad, small = feed_forward(
        hidden, normed, inv_std, output_grad, up_weight, up_bias, down_weight,
        first_gain, first_shift, down_bias, second_gain, second_shift,
    )
    dq, dk, dv, out_grad, pair_grad, small, up_grad, down_grad = attend_back(
        branch, out_weight, expon, inverse, q, k, v, attended, small, up_grad, down_grad, gathered
    )
    tokens_grad, out_grad, pair_grad, last_grad, bias_grads, up_grad = input_back(
        dq, dk, dv, query_weight, key_weight, value_weight, gathered, resid_grad, out_grad, pair_grad,
        up_grad,
    )

    up_grad, down_grad, out_grad, query_grad, key_grad, value_grad = widen_grads(
        up_grad, down_grad, out_grad, pair_grad, last_grad
    )
    return (
        layer_out,
        tokens_grad,
        query_grad,
        bias_grads[0],
        key_grad,
        value_grad,
        bias_grads[1],
        out_grad,
        small[5],
        small[3],
        small[4],
        up_grad,
        small[6],
        down_grad,
        small[2],
        small[0],
        small[1],
    )


def solution(mesh):
    placed = (
        P(("dp", "mp"), None),
        P("dp", None),
        P(None, "mp"),
        P("mp"),
        P(None, "mp"),
        P(None, "mp"),
        P("mp"),
        P("mp", None),
        P(),
        P(),
        P(),
        P(None, "mp"),
        P("mp"),
        P("mp", None),
        P(),
        P(),
        P(),
        P(("dp", "mp"), None),
    )
    return jax.shard_map(
        per_device,
        mesh=mesh,
        in_specs=placed,
        out_specs=(
            P(("dp", "mp"), None),
            P(("dp", "mp"), None),
            P(None, "mp"),
            P("mp"),
            P(None, "mp"),
            P(None, "mp"),
            P("mp"),
            P("mp", None),
            P(),
            P(),
            P(),
            P(None, "mp"),
            P("mp"),
            P("mp", None),
            P(),
            P(),
            P(),
        ),
        check_vma=False,
    )
```

profile of v0, /device:TPU:0, one launch (start us, length us, event | category | flops | bytes accessed | tf_op | source)
XLA Modules:
  0.0 350.9 jit_solution(3960750568366260138)
XLA Ops:
  1.3 33.9 %gather_project.1 = (bf16[2048,256]{1,0:T(8,128)(2,1)}, bf16[2048,256]{1,0:T(8,128)(2,1)}, bf16[2048,256]{1,0:T(8,128)(2,1)}, bf16[256,2048]{1,0:T(8,128)(2,1)}, bf16[4,512,1024]{2,1,0:T(8,128)(2,1)}) custom-call(bf16[512,1024]{1,0:T(8,128)(2,1)} %x_ref.3, bf16[1024,256]{1,0:T(8,128)(2,1)} %wq_ref.3, bf16[1024,256]{1,0:T(8,128)(2,1)} %wk_ref.3, ...), custom_call_target="tpu_custom_call" | custom-call | tf_op jit(solution)/shard_map/gather_project/pallas_call | solution.py:755
  35.2 41.5 %attend.1 = (bf16[8,4,2048,256]{3,2,1,0:T(8,128)(2,1)}, bf16[2048,256]{1,0:T(8,128)(2,1)}, f32[8,4,1,256]{3,2,1,0:T(1,128)}, f32[512,1024]{1,0:T(8,128)}, f32[512,1]{1,0:T(8,128)}, /*index=5*/bf16[512,1024]{1,0:T(8,128)(2,1)}) custom-call(s32[1,1]{1,0:T(1,128)S(6)} %copy.37.len_ref, bf16[2048,256]{1,0:T(8,128)(2,1)} %get-tuple-element.54.q_ref, ...), custom_call_target="tpu_custom_call" | custom-call | tf_op jit(solution)/shard_map/attend/pallas_call | solution.py:873
  76.7 117.1 %feed_forward.1 = (bf16[512,1024]{1,0:T(8,128)(2,1)}, bf16[512,1024]{1,0:T(8,128)(2,1)}, f32[512,1024]{1,0:T(8,128)}, bf16[1024,1024]{1,0:T(8,128)(2,1)}, bf16[1024,1024]{1,0:T(8,128)(2,1)}, /*index=5*/f32[8,1024]{1,0:T(8,128)}) custom-call(bf16[512,1024]{1,0:T(8,128)(2,1)} %get-tuple-element.57.h_ref, f32[512,1024]{1,0:T(8,128)} %get-tuple-element.58.n_ref, ...), custom_call_target="tpu_custom_call" | custom-call | tf_op jit(solution)/shard_map/feed_forward/pallas_call | solution.py:1115
  193.8 71.4 %attend_back.1 = (bf16[2048,256]{1,0:T(8,128)(2,1)}, bf16[2048,256]{1,0:T(8,128)(2,1)}, bf16[2048,256]{1,0:T(8,128)(2,1)}, bf16[256,1024]{1,0:T(8,128)(2,1)}, bf...) custom-call(bf16[512,1024]{1,0:T(8,128)(2,1)} %get-tuple-element.61.b_ref,, ...), custom_call_target="tpu_custom_call" | custom-call | tf_op jit(solution)/shard_map/attend_back/pallas_call | solution.py:1365
  265.2 0.0 copy-start.2
  265.2 72.4 %input_back.1 = (bf16[512,1024]{1,0:T(8,128)(2,1)}, bf16[256,1024]{1,0:T(8,128)(2,1)}, bf16[1024,384]{1,0:T(8,128)(2,1)}, bf16[1024,384]{1,0:T(8,128)(2,1)}, f32...) custom-call(bf16[2048,256]{1,0:T(8,128)(2,1)} %get-tuple-element.70.dq_ref, bf16[2048,256]{1,0:T(8,128)(2,1)} %get-tuple-element.71.dk_ref, ...), custom_call_target="tpu_custom_call" | custom-call | tf_op jit(solution)/shard_map/input_back/pallas_call | solution.py:1539
  337.7 1.3 fusion.1
  339.0 0.0 copy-done.2
  339.0 0.6 fusion
  339.6 0.0 copy-start
  339.6 8.6 %widen_grads.1 = (f32[1024,1024]{1,0:T(8,128)}, f32[1024,1024]{1,0:T(8,128)}, f32[256,1024]{1,0:T(8,128)}, f32[1024,256]{1,0:T(8,128)}, f32[1024,256]{1,0:T(8,128)}, /*index=5*/f32[1024,256]{1,0:T(8,128)}) custom-call(bf16[1024,1024]{1,0:T(8,128)(2,1)} %get-tuple-element.78.up_ref, bf16[1024,1024]{1,0:T(8,128)(2,1)} %get-tuple-element.79.down_ref, ...), custom_call_target="tpu_custom_call" | custom-call | tf_op jit(solution)/shard_map/widen_grads/pallas_call | solution.py:1591
  348.3 0.0 copy-start.1
  348.3 0.0 copy-done
  348.3 1.0 copy.38
  349.3 0.6 copy-done.1
  349.9 1.0 copy.39
Async XLA Ops:
  265.2 73.8 %copy-start.2 = (f32[8,1024]{1,0:T(8,128)S(1)}, f32[8,1024]{1,0:T(8,128)}, u32[]{:S(2)}) copy-start(f32[8,1024]{1,0:T(8,128)} %get-tuple-element.88) | copy-start | bytes 98308
  339.6 8.7 %copy-start = (bf16[512,1024]{1,0:T(8,128)(2,1)S(1)}, bf16[512,1024]{1,0:T(8,128)(2,1)}, u32[]{:S(2)}) copy-start(bf16[512,1024]{1,0:T(8,128)(2,1)} %get-tuple-element.117) | copy-start | bytes 3145732
  348.3 1.6 copy-start.1
where the time goes:
time: 351 us
  Pallas kernels  345 us (98%)
  local copies, waits for them, and re-layouts  4.53 us (1%)
    pallas_call x1, Pallas kernels, feed_forward(): pl.pallas_call(feed_forward_kernel, in_specs=[pl.BlockSpec(memory_space=p...  117 us
    pallas_call x1, Pallas kernels, input_back(): pl.pallas_call(input_back_kernel, in_specs=[WHOLE] * 10 + [pl.BlockSpec(m...  72.4 us
    pallas_call x1, Pallas kernels, attend_back(): pl.pallas_call(attend_back_kernel, grid=(4 * pairs,), in_specs=[anywhere,...  71.4 us
    pallas_call x1, Pallas kernels, attend(): pl.pallas_call(attend_kernel, grid=(steps,), in_specs=[pl.BlockSpec(memor...  41.5 us
    pallas_call x1, Pallas kernels, gather_project(): pl.pallas_call(project_kernel, in_specs=[pl.BlockSpec(memory_space=pl.ANY...  33.9 us
    pallas_call x1, Pallas kernels, widen_grads(): pl.pallas_call(widen_kernel, grid=(steps,), in_specs=[tiles(g.shape) for...  8.64 us

commit v1 on v0

--- a/solution.py
+++ b/solution.py
@@ -695,9 +695,7 @@
     return jnp.mean(value, -1, keepdims=True)
 
 
-def project_kernel(
-    x_ref, wq_ref, wk_ref, wv_ref, qb_ref, vb_ref, q_ref, k_ref, v_ref, vt_ref, all_ref, land, send, recv, save
-):
+def project(x_ref, wq_ref, wk_ref, wv_ref, qb_ref, vb_ref, q_ref, k_ref, v_ref, vt_ref, land, send, recv, save):
     rows_here = land.shape[1]
     load = pltpu.make_async_copy(x_ref, land.at[0], save.at[0])
     load.start()
@@ -707,10 +705,6 @@
     repeat(CHUNKS, gather.start)
     size = gather.size
 
-    def store(s, j):
-        rows = pl.ds(pl.multiple_of(j * size, size), size)
-        return pltpu.make_async_copy(land.at[s, rows], all_ref.at[s, rows], save.at[1 + s * CHUNKS + j])
-
     def emit(x, at):
         rows = pl.ds(pl.multiple_of(at, x.shape[0]), x.shape[0])
         q = (mm(x, wq_ref[...], 1, 0) + as_row(qb_ref)).astype(BF)
@@ -729,8 +723,6 @@
             gather.arrive(1, j + 1)
 
         emit(land[s, pl.ds(pl.multiple_of(j * size, 2 * size), 2 * size)], i * 2 * size)
-        store(s, j).start()
-        store(s, j + 1).start()
 
     repeat(4, close)
 
@@ -740,31 +732,11 @@
 
         def one(k):
             emit(land[2 + k, pl.ds(pl.multiple_of(j * size, size), size)], (2 + k) * rows_here + j * size)
-            store(2 + k, j).start()
 
         repeat(2, one)
 
     repeat(CHUNKS, far)
     gather.drain()
-    repeat(4, lambda s: repeat(CHUNKS, lambda j: store(s, j).wait()))
-
-
-def gather_project(tokens, wq, wk, wv, q_bias, v_bias):
-    rows, width = tokens.shape
-    cols = wq.shape[1]
-    return pl.pallas_call(
-        project_kernel,
-        in_specs=[pl.BlockSpec(memory_space=pl.ANY)] + [WHOLE] * 5,
-        out_specs=[WHOLE] * 4 + [pl.BlockSpec(memory_space=pl.ANY)],
-        out_shape=[shaped(4 * rows, cols)] * 3 + [shaped(cols, 4 * rows), shaped(4, rows, width)],
-        scratch_shapes=[
-            pltpu.VMEM((4, rows, width), BF),
-            *transfer_sems(),
-            pltpu.SemaphoreType.DMA((4 * CHUNKS + 1,)),
-        ],
-        name="gather_project",
-        compiler_params=comm_params(0),
-    )(tokens, wq, wk, wv, q_bias, v_bias)
 
 
 HALVES = 2
@@ -777,23 +749,36 @@
 
 
 def attend_kernel(
-    len_ref, q_ref, k_ref, vt_ref, w_ref, x_ref, ob_ref, gain_ref, shift_ref,
-    e_ref, o_ref, r_ref, n_ref, i_ref, h_ref,
+    len_ref, x_ref, wq_ref, wk_ref, wv_ref, qb_ref, vb_ref, w_ref, ob_ref, gain_ref, shift_ref,
+    q_out, k_out, v_out, all_out, e_ref, o_ref, r_ref, n_ref, i_ref, h_ref,
+    tokens, q_ref, k_ref, v_ref, vt_ref, gather_send, gather_recv, save,
     k_aug, v_aug, out, land, mine, pending, send, recv,
 ):
     step = pl.program_id(0)
-    seq_len, block = k_ref.shape[0], q_ref.shape[0]
+    seq_len, block = k_ref.shape[0], pending.shape[0]
+    rows_here = tokens.shape[1]
+    saves = [
+        pltpu.make_async_copy(src, dst, save.at[1 + i])
+        for i, (src, dst) in enumerate(
+            ((q_ref, q_out), (k_ref, k_out), (v_ref, v_out), (tokens, all_out))
+        )
+    ]
     pairs = k_ref.shape[1] // WIDE
     reduce = Reduce(out, land, send, recv, HALVES)
 
     @pl.when(step == 0)
     def _():
-        greet([mp_peer(1), mp_peer(2)])
+        project(
+            x_ref, wq_ref, wk_ref, wv_ref, qb_ref, vb_ref, q_ref, k_ref, v_ref, vt_ref,
+            tokens, gather_send, gather_recv, save,
+        )
+        for each in saves:
+            each.start()
         lanes = lax.broadcasted_iota(jnp.int32, (seq_len, WIDE), 1)
-        rows = lax.broadcasted_iota(jnp.int32, (x_ref.shape[0], WIDE), 0)
+        rows = lax.broadcasted_iota(jnp.int32, (rows_here, WIDE), 0)
         bias = jnp.concatenate(
             [
-                jnp.where(rows + mp_peer(s)[1] * x_ref.shape[0] < len_ref[0, 0], 0.0, MASKED)
+                jnp.where(rows + mp_peer(s)[1] * rows_here < len_ref[0, 0], 0.0, MASKED)
                 for s in range(4)
             ],
             0,
@@ -810,9 +795,10 @@
                 v_aug[2 * p + h, HD:] = jnp.ones((16, seq_len), BF)
 
     lanes = lax.broadcasted_iota(jnp.int32, (block, WIDE), 1)
+    q_rows = pl.ds(pl.multiple_of(forward_order(step) * block, block), block)
     outs = []
     for p in range(pairs):
-        query = q_ref[:, p * WIDE : (p + 1) * WIDE].astype(F32)
+        query = q_ref[q_rows, p * WIDE : (p + 1) * WIDE].astype(F32)
         scores = []
         for h in range(2):
             other = (1 - h) * HD
@@ -850,7 +836,7 @@
     def _():
         for j in range(HALVES):
             rows = pl.ds(j * block, block)
-            resid = x_ref[rows].astype(F32) + reduce.total(j, mine[rows]) + as_row(ob_ref)
+            resid = tokens[0, rows].astype(F32) + reduce.total(j, mine[rows]) + as_row(ob_ref)
             center = resid - row_mean(resid)
             inv_std = lax.rsqrt(row_mean(center * center) + epsilon)
             normed = center * inv_std
@@ -858,11 +844,13 @@
             i_ref[rows] = inv_std
             h_ref[rows] = (normed * as_row(gain_ref) + as_row(shift_ref)).astype(BF)
         reduce.drain()
-
-
-def attend(lengths, q, k, vt, out_weight, tokens, *vectors):
-    all_rows, cols = q.shape
+        for each in saves:
+            each.wait()
+
+
+def attend(lengths, tokens, wq, wk, wv, q_bias, v_bias, out_weight, *vectors):
     rows, width = tokens.shape
+    all_rows, cols = 4 * rows, wq.shape[1]
     block = rows // HALVES
     heads = cols // HD
     steps = all_rows // block
@@ -870,19 +858,20 @@
     def fixed(*shape):
         return pl.BlockSpec(shape, lambda i: (0,) * len(shape))
 
+    anywhere = pl.BlockSpec(memory_space=pl.ANY)
     return pl.pallas_call(
         attend_kernel,
         grid=(steps,),
         in_specs=[
             pl.BlockSpec(memory_space=pltpu.SMEM),
-            pl.BlockSpec((block, cols), lambda i: (forward_order(i), 0)),
-            fixed(all_rows, cols),
-            fixed(cols, all_rows),
+            anywhere,
+            *[fixed(width, cols)] * 3,
+            *[fixed(cols)] * 2,
             fixed(cols, width),
-            fixed(rows, width),
             *[fixed(width)] * 3,
         ],
         out_specs=[
+            *[anywhere] * 4,
             pl.BlockSpec((1, heads, all_rows, block), lambda i: (forward_order(i), 0, 0, 0)),
             pl.BlockSpec((block, cols), lambda i: (forward_order(i), 0)),
             pl.BlockSpec((1, heads, 1, block), lambda i: (forward_order(i), 0, 0, 0)),
@@ -891,6 +880,8 @@
             fixed(rows, width),
         ],
         out_shape=[
+            *[shaped(all_rows, cols)] * 3,
+            shaped(4, rows, width),
             shaped(steps, heads, all_rows, block),
             shaped(all_rows, cols),
             shaped(steps, heads, 1, block, dtype=F32),
@@ -899,6 +890,11 @@
             shaped(rows, width),
         ],
         scratch_shapes=[
+            pltpu.VMEM((4, rows, width), BF),
+            *[pltpu.VMEM((all_rows, cols), BF)] * 3,
+            pltpu.VMEM((cols, all_rows), BF),
+            *transfer_sems(),
+            pltpu.SemaphoreType.DMA((5,)),
             pltpu.VMEM((heads, all_rows, WIDE), BF),
             pltpu.VMEM((heads, HD + 16, all_rows), BF),
             pltpu.VMEM((3, rows, width), BF),
@@ -909,7 +905,7 @@
         ],
         name="attend",
         compiler_params=comm_params(1),
-    )(lengths, q, k, vt, out_weight, tokens, *vectors)
+    )(lengths, tokens, wq, wk, wv, q_bias, v_bias, out_weight, *vectors)
 
 
 ROOT_HALF = 0.7071067811865476
@@ -917,18 +913,26 @@
 
 
 def feed_forward_kernel(
-    h_ref, n_ref, i_ref, g_ref, up_ref, ub_ref, down_ref, *refs
+    h_ref, n_in, i_ref, g_in, up_in, ub_ref, down_in, *refs
 ):
     vectors, refs = refs[:5], refs[5:]
     (
-        out_ref, b1_ref, r1_ref, upg_ref, downg_ref, small_ref,
+        out_hbm, b1_ref, r1_ref, upg_hbm, downg_ref, small_ref,
         hidden, act, slope, branch, out1, land1, out2, land2, mine, pending, r2,
         gs1, gr1, gs2, gr2, rs1, rr1, rs2, rr2,
-        down_land, down_send, down_recv, load,
+        down_land, down_send, down_recv, load, n_ref, g_ref, up_ref, down_ref, out_ref, upg_ref,
     ) = refs
     rows_here, width = h_ref.shape
     fetch = pltpu.make_async_copy(h_ref, hidden.at[0], load.at[0])
     fetch.start()
+    fetches = [
+        pltpu.make_async_copy(src, dst, load.at[1 + i])
+        for i, (src, dst) in enumerate(
+            ((up_in, up_ref), (down_in, down_ref), (n_in, n_ref), (g_in, g_ref))
+        )
+    ]
+    save_out = pltpu.make_async_copy(out_ref, out_hbm, load.at[5])
+    save_upg = pltpu.make_async_copy(upg_ref, upg_hbm, load.at[6])
     size = rows_here // CHUNKS
     first_gain, first_shift, down_bias, second_gain, second_shift = map(as_row, vectors)
     greet_all()
@@ -937,6 +941,10 @@
     reduce1, reduce2 = Reduce(out1, land1, rs1, rr1), Reduce(out2, land2, rs2, rr2)
     fetch.wait()
     repeat(CHUNKS, gather1.start)
+    for each in fetches:
+        each.start()
+    for each in fetches[:2]:
+        each.wait()
     small_ref[...] = jnp.zeros_like(small_ref)
 
     def forward(x):
@@ -1018,7 +1026,10 @@
         branch[0, rows] = back.astype(BF)
         gather2.start(j)
 
+    for each in fetches[2:]:
+        each.wait()
     repeat(CHUNKS, second_norm)
+    save_out.start()
 
     def close_backward(i):
         s, half = i // 2, i % 2
@@ -1082,6 +1093,7 @@
     repeat(2, lambda t: down_grad(t + 2))
     advance((down_sum, (2, 3), 0))
     repeat(width // tile, up_grad)
+    save_upg.start()
 
     def first_norm(j):
         rows = chunk_rows(j)
@@ -1106,16 +1118,19 @@
     advance((down_sum, (0, 1, 2, 3), 3))
     for transfer in (gather1, gather2, reduce1, reduce2):
         transfer.drain()
+    save_out.wait()
+    save_upg.wait()
 
 
 def feed_forward(hidden, normed, inv_std, output_grad, up, up_bias, down, *vectors):
     rows, width = hidden.shape
     units = up.shape[1]
     tall = (4, rows, units)
+    anywhere = pl.BlockSpec(memory_space=pl.ANY)
     return pl.pallas_call(
         feed_forward_kernel,
-        in_specs=[pl.BlockSpec(memory_space=pl.ANY)] + [WHOLE] * 11,
-        out_specs=[WHOLE] * 6,
+        in_specs=[anywhere, anywhere, WHOLE, anywhere, anywhere, WHOLE, anywhere] + [WHOLE] * 5,
+        out_specs=[anywhere, WHOLE, WHOLE, anywhere, WHOLE, WHOLE],
         out_shape=[
             shaped(rows, width),
             shaped(rows, width),
@@ -1137,7 +1152,13 @@
             *transfer_sems(),
             spread_land((units, width), KINDS),
             *spread_sems(KINDS),
-            pltpu.SemaphoreType.DMA((1,)),
+            pltpu.SemaphoreType.DMA((7,)),
+            pltpu.VMEM((rows, width), F32),
+            pltpu.VMEM((rows, width), BF),
+            pltpu.VMEM((width, units), BF),
+            pltpu.VMEM((units, width), BF),
+            pltpu.VMEM((rows, width), BF),
+            pltpu.VMEM((width, units), BF),
         ],
         name="feed_forward",
         compiler_params=comm_params(2),
@@ -1582,7 +1603,7 @@
 
 
 def widen_grads(*grads):
-    steps = 8
+    steps = 4
     shapes = [g.shape for g in grads[:3]] + [(grads[3].shape[0], 2 * WIDE)] * 3
 
     def tiles(shape):
@@ -1610,11 +1631,9 @@
             out_weight, out_bias, first_gain, first_shift, up_weight, up_bias, down_weight,
             down_bias, second_gain, second_shift, output_grad,
         )
-    q, k, v, vt, gathered = gather_project(
-        tokens, query_weight, key_weight, value_weight, query_bias, value_bias
-    )
-    expon, attended, inverse, normed, inv_std, hidden = attend(
-        lengths, q, k, vt, out_weight, tokens, out_bias, first_gain, first_shift
+    q, k, v, gathered, expon, attended, inverse, normed, inv_std, hidden = attend(
+        lengths, tokens, query_weight, key_weight, value_weight, query_bias, value_bias, out_weight,
+        out_bias, first_gain, first_shift,
     )
     layer_out, branch, resid_grad, up_grad, down_grad, small = feed_forward(
         hidden, normed, inv_std, output_grad, up_weight, up_bias, down_weight,

time: 351 us -> 345 us (0.983)
  Pallas kernels: 345 us -> 338 us
    pallas_call x2 -> x1, Pallas kernels: 151 us -> 115 us  [feed_forward(): pl.pallas_call(feed_forward_kernel, in_specs=[anywhere, anywhere, WHOLE,...]
    pallas_call x1, Pallas kernels: 41.5 us -> 70.7 us  [attend(): pl.pallas_call(attend_kernel, grid=(steps,), in_specs=[pl.BlockSpec(memor...]
where the time goes in v1:
time: 345 us; the launch traced here: 344 us
  Pallas kernels  338 us (98%)
  local copies, waits for them, and re-layouts  4.53 us (1%)
    pallas_call x1, Pallas kernels, feed_forward(): pl.pallas_call(feed_forward_kernel, in_specs=[anywhere, anywhere, WHOLE,...  115 us
    pallas_call x1, Pallas kernels, input_back(): pl.pallas_call(input_back_kernel, in_specs=[WHOLE] * 10 + [pl.BlockSpec(m...  73.1 us
    pallas_call x1, Pallas kernels, attend_back(): pl.pallas_call(attend_back_kernel, grid=(4 * pairs,), in_specs=[anywhere,...  72.1 us
    pallas_call x1, Pallas kernels, attend(): pl.pallas_call(attend_kernel, grid=(steps,), in_specs=[pl.BlockSpec(memor...  70.7 us
    pallas_call x1, Pallas kernels, widen_grads(): pl.pallas_call(widen_kernel, grid=(steps,), in_specs=[tiles(g.shape) for...  7.59 us

profile of v1, /device:TPU:0, one launch (start us, length us, event | category | flops | bytes accessed | tf_op | source)
XLA Modules:
  0.0 344.2 jit_solution(2519012594897145241)
XLA Ops:
  1.3 70.7 %attend.1 = (bf16[2048,256]{1,0:T(8,128)(2,1)}, bf16[2048,256]{1,0:T(8,128)(2,1)}, bf16[2048,256]{1,0:T(8,128)(2,1)}, bf16[4,512,1024]{2,1,0:T(8,128)(2,1)}, bf1...) custom-call(s32[1,1]{1,0:T(1,128)S(6)} %copy.37.len_ref, ...), custom_call_target="tpu_custom_call" | custom-call | tf_op jit(solution)/shard_map/attend/pallas_call | solution.py:862
  72.0 114.9 %feed_forward.1 = (bf16[512,1024]{1,0:T(8,128)(2,1)}, bf16[512,1024]{1,0:T(8,128)(2,1)}, f32[512,1024]{1,0:T(8,128)}, bf16[1024,1024]{1,0:T(8,128)(2,1)}, bf16[1024,1024]{1,0:T(8,128)(2,1)}, /*index=5*/f32[8,1024]{1,0:T(8,128)}) custom-call(bf16[512,1024]{1,0:T(8,128)(2,1)} %get-tuple-element.53.h_ref, f32[512,1024]{1,0:T(8,128)} %get-tuple-element.54.n_in, ...), custom_call_target="tpu_custom_call" | custom-call | tf_op jit(solution)/shard_map/feed_forward/pallas_call | solution.py:1130
  186.9 72.1 %attend_back.1 = (bf16[2048,256]{1,0:T(8,128)(2,1)}, bf16[2048,256]{1,0:T(8,128)(2,1)}, bf16[2048,256]{1,0:T(8,128)(2,1)}, bf16[256,1024]{1,0:T(8,128)(2,1)}, bf...) custom-call(bf16[512,1024]{1,0:T(8,128)(2,1)} %get-tuple-element.57.b_ref,, ...), custom_call_target="tpu_custom_call" | custom-call | tf_op jit(solution)/shard_map/attend_back/pallas_call | solution.py:1386
  259.0 0.0 copy-start.2
  259.0 73.1 %input_back.1 = (bf16[512,1024]{1,0:T(8,128)(2,1)}, bf16[256,1024]{1,0:T(8,128)(2,1)}, bf16[1024,384]{1,0:T(8,128)(2,1)}, bf16[1024,384]{1,0:T(8,128)(2,1)}, f32...) custom-call(bf16[2048,256]{1,0:T(8,128)(2,1)} %get-tuple-element.68.dq_ref, bf16[2048,256]{1,0:T(8,128)(2,1)} %get-tuple-element.69.dk_ref, ...), custom_call_target="tpu_custom_call" | custom-call | tf_op jit(solution)/shard_map/input_back/pallas_call | solution.py:1560
  332.1 1.3 fusion.1
  333.4 0.0 copy-done.2
  333.4 0.6 fusion
  334.0 0.0 copy-start
  334.0 7.6 %widen_grads.1 = (f32[1024,1024]{1,0:T(8,128)}, f32[1024,1024]{1,0:T(8,128)}, f32[256,1024]{1,0:T(8,128)}, f32[1024,256]{1,0:T(8,128)}, f32[1024,256]{1,0:T(8,128)}, /*index=5*/f32[1024,256]{1,0:T(8,128)}) custom-call(bf16[1024,1024]{1,0:T(8,128)(2,1)} %get-tuple-element.76.up_ref, bf16[1024,1024]{1,0:T(8,128)(2,1)} %get-tuple-element.77.down_ref, ...), custom_call_target="tpu_custom_call" | custom-call | tf_op jit(solution)/shard_map/widen_grads/pallas_call | solution.py:1612
  341.6 0.0 copy-start.1
  341.6 0.0 copy-done
  341.6 1.0 copy.38
  342.6 0.6 copy-done.1
  343.2 1.0 copy.39
Async XLA Ops:
  259.0 74.4 %copy-start.2 = (f32[8,1024]{1,0:T(8,128)S(1)}, f32[8,1024]{1,0:T(8,128)}, u32[]{:S(2)}) copy-start(f32[8,1024]{1,0:T(8,128)} %get-tuple-element.86) | copy-start | bytes 98308
  334.0 7.6 %copy-start = (bf16[512,1024]{1,0:T(8,128)(2,1)S(1)}, bf16[512,1024]{1,0:T(8,128)(2,1)}, u32[]{:S(2)}) copy-start(bf16[512,1024]{1,0:T(8,128)(2,1)} %get-tuple-element.115) | copy-start | bytes 3145732
  341.6 1.6 copy-start.1

commit v2 on v1

--- a/solution.py
+++ b/solution.py
@@ -1449,10 +1449,10 @@
 
 
 def input_back_kernel(
-    dq_ref, dk_ref, dv_ref, wq_ref, wk_ref, wv_ref, all_ref, r1_ref, wg_in, pg_in, up_in,
+    dq_ref, dk_ref, dv_ref, wq_ref, wk_ref, wv_ref, all_in, r1_in, wg_in, pg_in, up_in,
     x_ref, wg_ref, pg_ref, last_ref, bias_ref, up_out,
     out, land, mine, pending, send, recv, up, loads, up_send, up_recv, out_send, out_recv,
-    pair_send, pair_recv, joint, w_full, p_full, last_full, last_low, last_land, last_send, last_recv,
+    pair_send, pair_recv, all_ref, r1_ref, joint, w_full, p_full, last_full, last_low, last_land, last_send, last_recv,
     value, bias_land, bias_send, bias_recv,
 ):
     rows_here = r1_ref.shape[0]
@@ -1469,8 +1469,12 @@
         pltpu.make_async_copy(up_in.at[up_sum.own(job)], up.at[up_sum.own(job)], loads.at[job])
         for job in range(JOBS)
     ]
+    load_all = pltpu.make_async_copy(all_in, all_ref, loads.at[JOBS + 1])
+    load_r1 = pltpu.make_async_copy(r1_in, r1_ref, loads.at[JOBS + 2])
     for load in load_up:
         load.start()
+    load_all.start()
+    load_r1.start()
     w_full[out_sum.own(0)] = wg_in[out_sum.own(0)]
     for job in range(JOBS):
         p_full[pair_sum.own(job)] = pg_in[pair_sum.own(job)]
@@ -1484,6 +1488,7 @@
     tail = pl.ds(last, WIDE)
     for at, grad in enumerate((dq_ref, dk_ref, dv_ref)):
         joint[:, at * WIDE : (at + 1) * WIDE] = grad[:, tail]
+    load_all.wait()
     projection_grads(all_ref, joint, last_low)
     advance((last_sum, (0, 1, 2, 3), 0))
     grads = ((dq_ref, wq_ref), (dk_ref, wk_ref), (dv_ref, wv_ref))
@@ -1532,6 +1537,7 @@
         x_ref[rows] = (r1_ref[rows] + reduce.total(j, mine[rows])).astype(BF)
 
     advance((pair_sum, (3, 0, 1, 2), 5), (up_sum, (1, 2), 4))
+    load_r1.wait()
     finish(0)
     bias.finish(1)
     bias.start(2)
@@ -1557,9 +1563,10 @@
 def input_back(dq, dk, dv, wq, wk, wv, gathered, resid_grad, out_grad, pair_grad, up):
     rows, width = resid_grad.shape
     cols = dq.shape[1]
+    anywhere = pl.BlockSpec(memory_space=pl.ANY)
     return pl.pallas_call(
         input_back_kernel,
-        in_specs=[WHOLE] * 10 + [pl.BlockSpec(memory_space=pl.ANY)],
+        in_specs=[WHOLE] * 6 + [anywhere] * 2 + [WHOLE] * 2 + [anywhere],
         out_specs=[WHOLE] * 5 + [pl.BlockSpec(memory_space=pl.ANY)],
         out_shape=[
             shaped(rows, width),
@@ -1576,10 +1583,12 @@
             pltpu.VMEM((rows, width), F32),
             *transfer_sems(),
             pltpu.VMEM(up.shape, BF),
-            pltpu.SemaphoreType.DMA((JOBS + 1,)),
+            pltpu.SemaphoreType.DMA((JOBS + 3,)),
             *spread_sems(KINDS),
             *spread_sems("H"),
             *spread_sems(KINDS),
+            pltpu.VMEM(gathered.shape, BF),
+            pltpu.VMEM((rows, width), F32),
             pltpu.VMEM((dq.shape[0], 3 * WIDE), BF),
             pltpu.VMEM(out_grad.shape, BF),
             *[pltpu.VMEM(pair_grad.shape, BF)] * 3,

time: 345 us -> 343 us (level)
  no operation moved by 1% of the time
where the time goes in v2:
time: 343 us; the launch traced here: 342 us
  Pallas kernels  337 us (98%)
  local copies, waits for them, and re-layouts  4.53 us (1%)
    pallas_call x1, Pallas kernels, feed_forward(): pl.pallas_call(feed_forward_kernel, in_specs=[anywhere, anywhere, WHOLE,...  115 us
    pallas_call x1, Pallas kernels, attend_back(): pl.pallas_call(attend_back_kernel, grid=(4 * pairs,), in_specs=[anywhere,...  72.1 us
    pallas_call x1, Pallas kernels, input_back(): pl.pallas_call(input_back_kernel, in_specs=[WHOLE] * 6 + [anywhere] * 2 +...  71.3 us
    pallas_call x1, Pallas kernels, attend(): pl.pallas_call(attend_kernel, grid=(steps,), in_specs=[pl.BlockSpec(memor...  70.7 us
    pallas_call x1, Pallas kernels, widen_grads(): pl.pallas_call(widen_kernel, grid=(steps,), in_specs=[tiles(g.shape) for...  7.59 us

profile of v2, /device:TPU:0, one launch (start us, length us, event | category | flops | bytes accessed | tf_op | source)
XLA Modules:
  0.0 342.4 jit_solution(9935577004485417156)
XLA Ops:
  1.3 70.7 %attend.1 = (bf16[2048,256]{1,0:T(8,128)(2,1)}, bf16[2048,256]{1,0:T(8,128)(2,1)}, bf16[2048,256]{1,0:T(8,128)(2,1)}, bf16[4,512,1024]{2,1,0:T(8,128)(2,1)}, bf1...) custom-call(s32[1,1]{1,0:T(1,128)S(6)} %copy.37.len_ref, ...), custom_call_target="tpu_custom_call" | custom-call | tf_op jit(solution)/shard_map/attend/pallas_call | solution.py:862
  72.0 114.9 %feed_forward.1 = (bf16[512,1024]{1,0:T(8,128)(2,1)}, bf16[512,1024]{1,0:T(8,128)(2,1)}, f32[512,1024]{1,0:T(8,128)}, bf16[1024,1024]{1,0:T(8,128)(2,1)}, bf16[1024,1024]{1,0:T(8,128)(2,1)}, /*index=5*/f32[8,1024]{1,0:T(8,128)}) custom-call(bf16[512,1024]{1,0:T(8,128)(2,1)} %get-tuple-element.53.h_ref, f32[512,1024]{1,0:T(8,128)} %get-tuple-element.54.n_in, ...), custom_call_target="tpu_custom_call" | custom-call | tf_op jit(solution)/shard_map/feed_forward/pallas_call | solution.py:1130
  186.9 72.1 %attend_back.1 = (bf16[2048,256]{1,0:T(8,128)(2,1)}, bf16[2048,256]{1,0:T(8,128)(2,1)}, bf16[2048,256]{1,0:T(8,128)(2,1)}, bf16[256,1024]{1,0:T(8,128)(2,1)}, bf...) custom-call(bf16[512,1024]{1,0:T(8,128)(2,1)} %get-tuple-element.57.b_ref,, ...), custom_call_target="tpu_custom_call" | custom-call | tf_op jit(solution)/shard_map/attend_back/pallas_call | solution.py:1386
  259.0 0.0 copy-start.2
  259.0 71.3 %input_back.1 = (bf16[512,1024]{1,0:T(8,128)(2,1)}, bf16[256,1024]{1,0:T(8,128)(2,1)}, bf16[1024,384]{1,0:T(8,128)(2,1)}, bf16[1024,384]{1,0:T(8,128)(2,1)}, f32...) custom-call(bf16[2048,256]{1,0:T(8,128)(2,1)} %get-tuple-element.68.dq_ref, bf16[2048,256]{1,0:T(8,128)(2,1)} %get-tuple-element.69.dk_ref, ...), custom_call_target="tpu_custom_call" | custom-call | tf_op jit(solution)/shard_map/input_back/pallas_call | solution.py:1567
  330.3 1.3 fusion.1
  331.6 0.0 copy-done.2
  331.6 0.6 fusion
  332.2 0.0 copy-start
  332.2 7.6 %widen_grads.1 = (f32[1024,1024]{1,0:T(8,128)}, f32[1024,1024]{1,0:T(8,128)}, f32[256,1024]{1,0:T(8,128)}, f32[1024,256]{1,0:T(8,128)}, f32[1024,256]{1,0:T(8,128)}, /*index=5*/f32[1024,256]{1,0:T(8,128)}) custom-call(bf16[1024,1024]{1,0:T(8,128)(2,1)} %get-tuple-element.76.up_ref, bf16[1024,1024]{1,0:T(8,128)(2,1)} %get-tuple-element.77.down_ref, ...), custom_call_target="tpu_custom_call" | custom-call | tf_op jit(solution)/shard_map/widen_grads/pallas_call | solution.py:1621
  339.8 0.0 copy-start.1
  339.8 0.0 copy-done
  339.8 1.0 copy.38
  340.8 0.6 copy-done.1
  341.4 1.0 copy.39
Async XLA Ops:
  259.0 72.6 %copy-start.2 = (f32[8,1024]{1,0:T(8,128)S(1)}, f32[8,1024]{1,0:T(8,128)}, u32[]{:S(2)}) copy-start(f32[8,1024]{1,0:T(8,128)} %get-tuple-element.86) | copy-start | bytes 98308
  332.2 7.6 %copy-start = (bf16[512,1024]{1,0:T(8,128)(2,1)S(1)}, bf16[512,1024]{1,0:T(8,128)(2,1)}, u32[]{:S(2)}) copy-start(bf16[512,1024]{1,0:T(8,128)(2,1)} %get-tuple-element.115) | copy-start | bytes 3145732
  339.8 1.6 copy-start.1
